TPU v7x, 8 devices: a whole 2x2x1 slice. The times are simulated.
8 devices in a mesh: cola: 2 (over z, y), colb: 2 (over x), row: 2 (over core).
Axes of the slice: x: 2, y: 2, z: 1, core: 2. Of those that a mesh axis runs over, the one named last changes fastest.
Arguments:
- inter_mask: int32 [32768, 8192], P('row', ('cola', 'colb'))
- user_emb: bfloat16 [32768, 256], P(('row', 'cola', 'colb'))
- item_emb: bfloat16 [8192, 256], P(('cola', 'colb', 'row'))
- triples: int32 [256, 3], replicated
Outputs:
- output 1: bfloat16 [32768, 256], P(('row', 'cola', 'colb'))
- output 2: bfloat16 [8192, 256], P(('cola', 'colb', 'row'))
- output 3: float32 [], replicated
All inputs are finite; a program needn't handle non-finite values.
Results may differ from a plain program's by a relative error of at most 0.00583716.
Values are sent between devices in bfloat16 or wider.
A program may use at most 1 GiB of HBM per device.

v0:
```python
import math
import jax
import jax.numpy as jnp
from jax import lax
from jax.sharding import PartitionSpec as P

LAYERS = 3
USER_AXES = ('row', 'cola', 'colb')
ITEM_AXES = ('cola', 'colb', 'row')
COL_AXES = ('cola', 'colb')
CONTRACT_ROWS = (((0,), (0,)), ((), ()))


def build_adjacency(mask_blk, deg_user, deg_item):
    user_scale = lax.rsqrt(jnp.maximum(deg_user, 1).astype(jnp.float32))
    item_scale = lax.rsqrt(jnp.maximum(deg_item, 1).astype(jnp.float32))
    weights = (user_scale[:, None] * mask_blk.astype(jnp.float32)) * item_scale[None, :]
    return weights.astype(jnp.bfloat16)


def owned_rows(emb_table, row_ids, owner_idx):
    shard_rows = emb_table.shape[0]
    is_owned = (row_ids // shard_rows) == owner_idx
    picked = jnp.take(emb_table, row_ids % shard_rows, axis=0).astype(jnp.float32)
    return jnp.where(is_owned[:, None], picked, 0.0)


def bpr_loss(fetched):
    user_rows = fetched[0]
    pos_rows = fetched[1]
    neg_rows = fetched[2]
    margin = (jnp.sum(user_rows * pos_rows, axis=1) - jnp.sum(user_rows * neg_rows, axis=1)) / math.sqrt(user_rows.shape[1])
    return jnp.mean(jax.nn.softplus(-margin))


def solution(mesh):
    row_count = mesh.shape['row']
    colb_count = mesh.shape['colb']
    col_count = mesh.shape['cola'] * colb_count

    def device_program(mask_blk, user_shard, item_shard, triples):
        row_idx = lax.axis_index('row')
        col_idx = lax.axis_index('cola') * colb_count + lax.axis_index('colb')
        deg_user = lax.psum(jnp.sum(mask_blk, axis=1), COL_AXES)
        deg_item = lax.psum(jnp.sum(mask_blk, axis=0), 'row')
        adjacency = build_adjacency(mask_blk, deg_user, deg_item)
        user_cur = user_shard
        item_cur = item_shard
        user_total = user_shard.astype(jnp.float32)
        item_total = item_shard.astype(jnp.float32)
        for layer_idx in range(LAYERS):
            item_panel = lax.all_gather(item_cur, 'row', axis=0, tiled=True)
            user_panel = lax.all_gather(user_cur, COL_AXES, axis=0, tiled=True)
            user_part = jnp.dot(adjacency, item_panel, preferred_element_type=jnp.float32)
            item_part = lax.dot_general(adjacency, user_panel, CONTRACT_ROWS, preferred_element_type=jnp.float32)
            user_cur = lax.psum_scatter(user_part, COL_AXES, scatter_dimension=0, tiled=True).astype(jnp.bfloat16)
            item_cur = lax.psum_scatter(item_part, 'row', scatter_dimension=0, tiled=True).astype(jnp.bfloat16)
            user_total = user_total + user_cur.astype(jnp.float32)
            item_total = item_total + item_cur.astype(jnp.float32)
        user_out = (user_total / (LAYERS + 1)).astype(jnp.bfloat16)
        item_out = (item_total / (LAYERS + 1)).astype(jnp.bfloat16)
        user_owner = row_idx * col_count + col_idx
        item_owner = col_idx * row_count + row_idx
        fetched = jnp.stack([owned_rows(user_out, triples[:, 0], user_owner), owned_rows(item_out, triples[:, 1], item_owner), owned_rows(item_out, triples[:, 2], item_owner)])
        loss = bpr_loss(lax.psum(fetched, USER_AXES))
        return user_out, item_out, loss

    return jax.shard_map(device_program, mesh=mesh, in_specs=(P('row', COL_AXES), P(USER_AXES, None), P(ITEM_AXES, None), P()), out_specs=(P(USER_AXES, None), P(ITEM_AXES, None), P()), check_vma=False)
```

profile of v0, /device:TPU:0, one launch (start us, length us, event | category | flops | bytes accessed | tf_op | source)
XLA Modules:
  0.0 1003.0 jit_solution(12043136494551930483)
XLA Ops:
  7.2 40.7 %fusion.5 = (s32[16384]{0:T(1024)}, s32[2048]{0:T(1024)S(1)}) fusion(s32[16384,2048]{1,0:T(8,128)} %param.6), kind=kLoop, calls=%fused_computation.52 | loop fusion | flops 67090432 | bytes 134291456 | tf_op jit(solution)/shard_map/reduce_sum | solution.py:44
  51.1 30.3 %all-reduce.3.cloned.1.call-done = s32[16384]{0:T(1024)} async-done(((s32[16384]{0:T(1024)}), s32[16384]{0:T(1024)}) %all-reduce.3.cloned.1.call-update) | async-done | bytes 65552 | tf_op jit(solution)/shard_map/psum | solution.py:44
  82.2 63.9 %multiply_convert_fusion = bf16[16384,2048]{1,0:T(8,128)(2,1)} fusion(s32[16384,2048]{1,0:T(8,128)} %param.6, f32[2048]{0:T(1024)S(1)} %convert_rsqrt_fusion.1, f32[16384]{0:T(1024)S(1)} %convert_rsqrt_fusion), kind=kLoop, calls=%fused_computation.3 | loop fusion | flops 134217728 | bytes 201400320 | tf_op jit(solution)/shard_map/convert_element_type | solution.py:18
  146.1 18.9 %all-gather.9.cloned.1.call-done = bf16[16384,256]{1,0:T(8,128)(2,1)} async-done(((bf16[4096,256]{1,0:T(8,128)(2,1)}), bf16[16384,256]{1,0:T(8,128)(2,1)}) %all-gather.9.cloned.1.call-update) | async-done | bytes 8388624 | tf_op jit(solution)/shard_map/all_gather | solution.py:53
  165.0 30.7 %fusion.8 = f32[2048,256]{1,0:T(8,128)} fusion(bf16[16384,2048]{1,0:T(8,128)(2,1)} %multiply_convert_fusion, bf16[16384,256]{1,0:T(8,128)(2,1)} %all-gather.9.cloned.1.call-done), kind=kOutput, calls=%fused_computation.55 | convolution fusion | flops 17179869184 | bytes 77594624 | tf_op jit(solution)/shard_map/dot_general | solution.py:55
  196.3 6.0 reduce-scatter.9.cloned.1.call-done
  204.5 6.5 all-gather.7.cloned.1.call-done
  211.0 30.9 %fusion.7 = f32[16384,256]{1,0:T(8,128)} fusion(bf16[16384,2048]{1,0:T(8,128)(2,1)} %multiply_convert_fusion, bf16[2048,256]{1,0:T(8,128)(2,1)} %all-gather.7.cloned.1.call-done), kind=kOutput, calls=%fused_computation.54 | convolution fusion | flops 17179869184 | bytes 84934656 | tf_op jit(solution)/shard_map/dot_general | solution.py:54
  242.2 31.0 %fusion.9 = f32[16384,256]{1,0:T(8,128)} fusion(bf16[16384,2048]{1,0:T(8,128)(2,1)} %multiply_convert_fusion, bf16[2048,256]{1,0:T(8,128)(2,1)} %all-gather.11.cloned.1.call-done), kind=kOutput, calls=%fused_computation.56 | convolution fusion | flops 17179869184 | bytes 84934656 | tf_op jit(solution)/shard_map/dot_general | solution.py:54
  273.2 118.0 %reduce-scatter.7.cloned.1.call-done = f32[4096,256]{1,0:T(8,128)} async-done(((f32[16384,256]{1,0:T(8,128)}), f32[4096,256]{1,0:T(8,128)}) %reduce-scatter.7.cloned.1.call-update) | async-done | bytes 4194320 | tf_op jit(solution)/shard_map/reduce_scatter | solution.py:56
  391.2 3.7 convert_element_type.81
  395.0 147.2 %reduce-scatter.11.cloned.1.call-done = f32[4096,256]{1,0:T(8,128)} async-done(((f32[16384,256]{1,0:T(8,128)}), f32[4096,256]{1,0:T(8,128)}) %reduce-scatter.11.cloned.1.call-update) | async-done | bytes 4194320 | tf_op jit(solution)/shard_map/reduce_scatter | solution.py:56
  542.2 3.7 convert_element_type.84
  546.0 79.9 %all-gather.13.cloned.1.call-done = bf16[16384,256]{1,0:T(8,128)(2,1)} async-done(((bf16[4096,256]{1,0:T(8,128)(2,1)}), bf16[16384,256]{1,0:T(8,128)(2,1)}) %all-gather.13.cloned.1.call-update) | async-done | bytes 8388624 | tf_op jit(solution)/shard_map/all_gather | solution.py:53
  625.8 30.7 %fusion.10 = f32[2048,256]{1,0:T(8,128)} fusion(bf16[16384,2048]{1,0:T(8,128)(2,1)} %multiply_convert_fusion, bf16[16384,256]{1,0:T(8,128)(2,1)} %all-gather.13.cloned.1.call-done), kind=kOutput, calls=%fused_computation.57 | convolution fusion | flops 17179869184 | bytes 77594624 | tf_op jit(solution)/shard_map/dot_general | solution.py:55
  656.6 53.4 %all-gather.17.cloned.1.call-done = bf16[16384,256]{1,0:T(8,128)(2,1)} async-done(((bf16[4096,256]{1,0:T(8,128)(2,1)}), bf16[16384,256]{1,0:T(8,128)(2,1)}) %all-gather.17.cloned.1.call-update) | async-done | bytes 8388624 | tf_op jit(solution)/shard_map/all_gather | solution.py:53
  710.0 30.7 %fusion.12 = f32[2048,256]{1,0:T(8,128)} fusion(bf16[16384,2048]{1,0:T(8,128)(2,1)} %multiply_convert_fusion, bf16[16384,256]{1,0:T(8,128)(2,1)} %all-gather.17.cloned.1.call-done), kind=kOutput, calls=%fused_computation.59 | convolution fusion | flops 17179869184 | bytes 77594624 | tf_op jit(solution)/shard_map/dot_general | solution.py:55
  741.0 6.4 reduce-scatter.17.cloned.1.call-done
  750.1 7.3 all-gather.15.cloned.1.call-done
  757.4 30.9 %fusion.11 = f32[16384,256]{1,0:T(8,128)} fusion(bf16[16384,2048]{1,0:T(8,128)(2,1)} %multiply_convert_fusion, bf16[2048,256]{1,0:T(8,128)(2,1)} %all-gather.15.cloned.1.call-done), kind=kOutput, calls=%fused_computation.58 | convolution fusion | flops 17179869184 | bytes 84934656 | tf_op jit(solution)/shard_map/dot_general | solution.py:54
  791.7 146.0 %reduce-scatter.15.cloned.1.call-done = f32[4096,256]{1,0:T(8,128)} async-done(((f32[16384,256]{1,0:T(8,128)}), f32[4096,256]{1,0:T(8,128)}) %reduce-scatter.15.cloned.1.call-update) | async-done | bytes 4194320 | tf_op jit(solution)/shard_map/reduce_scatter | solution.py:56
  937.7 7.0 multiply_convert_fusion.1
  944.6 2.8 gather_fusion
  948.6 44.2 %all-reduce.5.cloned.1.call-done = f32[3,256,256]{2,1,0:T(8,128)} async-done(((f32[3,256,256]{2,1,0:T(8,128)}), f32[3,256,256]{2,1,0:T(8,128)}) %all-reduce.5.cloned.1.call-update) | async-done | bytes 786448 | tf_op jit(solution)/shard_map/psum | solution.py:65
  (60 shorter events, 16.5 us)
Async XLA Ops:
  7.2 74.2 %all-reduce.3.cloned.1.call-start = ((), (), s32[]{:S(2)}) async-start(), calls=%async_computation.6 | async-start | bytes 131072 | tf_op jit(solution)/shard_map/psum | solution.py:44
  47.9 117.1 %all-gather.9.cloned.1.call-start = ((), (), s32[]{:S(2)}) async-start(), calls=%async_computation.9 | async-start | bytes 10485760 | tf_op jit(solution)/shard_map/all_gather | solution.py:53
  48.7 153.7 %reduce-scatter.9.cloned.1.call-start = ((), (), s32[]{:S(2)}) async-start(), calls=%async_computation.10 | async-start | bytes 3145728 | tf_op jit(solution)/shard_map/reduce_scatter | solution.py:57
  195.7 15.3 %all-gather.7.cloned.1.call-start = ((), (), s32[]{:S(2)}) async-start(), calls=%async_computation.7 | async-start | bytes 1572864 | tf_op jit(solution)/shard_map/all_gather | solution.py:52
  196.3 45.9 %all-gather.11.cloned.1.call-start = ((), (), s32[]{:S(2)}) async-start(), calls=%async_computation.11 | async-start | bytes 1572864 | tf_op jit(solution)/shard_map/all_gather | solution.py:52
  204.5 186.7 %reduce-scatter.7.cloned.1.call-start = ((), (), s32[]{:S(2)}) async-start(), calls=%async_computation.8 | async-start | bytes 20971520 | tf_op jit(solution)/shard_map/reduce_scatter | solution.py:56
  241.9 300.2 %reduce-scatter.11.cloned.1.call-start = ((), (), s32[]{:S(2)}) async-start(), calls=%async_computation.12 | async-start | bytes 20971520 | tf_op jit(solution)/shard_map/reduce_scatter | solution.py:56
  273.2 352.6 %all-gather.13.cloned.1.call-start = ((), (), s32[]{:S(2)}) async-start(), calls=%async_computation.13 | async-start | bytes 10485760 | tf_op jit(solution)/shard_map/all_gather | solution.py:53
  395.0 315.1 %all-gather.17.cloned.1.call-start = ((), (), s32[]{:S(2)}) async-start(), calls=%async_computation.17 | async-start | bytes 10485760 | tf_op jit(solution)/shard_map/all_gather | solution.py:53
  545.9 195.1 %reduce-scatter.13.cloned.1.call-start = ((), (), s32[]{:S(2)}) async-start(), calls=%async_computation.14 | async-start | bytes 3145728 | tf_op jit(solution)/shard_map/reduce_scatter | solution.py:57
  656.5 90.9 %copy-start.2 = (f32[1024,256]{1,0:T(8,128)S(1)}, f32[1024,256]{1,0:T(8,128)}, u32[]{:S(2)}) copy-start(f32[1024,256]{1,0:T(8,128)} %reduce-scatter.9.cloned.1.call-done) | copy-start | bytes 3145732
  656.5 90.9 %copy-start.3 = (bf16[1024,256]{1,0:T(8,128)(2,1)S(1)}, bf16[1024,256]{1,0:T(8,128)(2,1)}, u32[]{:S(2)}) copy-start(bf16[1024,256]{1,0:T(8,128)(2,1)} %param.8) | copy-start | bytes 1572868
  656.5 90.9 %reduce-scatter.17.cloned.1.call-start = ((), (), s32[]{:S(2)}) async-start(), calls=%async_computation.18 | async-start | bytes 3145728 | tf_op jit(solution)/shard_map/reduce_scatter | solution.py:57
  740.7 16.7 %all-gather.15.cloned.1.call-start = ((), (), s32[]{:S(2)}) async-start(), calls=%async_computation.15 | async-start | bytes 1572864 | tf_op jit(solution)/shard_map/all_gather | solution.py:52
  750.0 40.3 %copy-start = (bf16[1024,256]{1,0:T(8,128)(2,1)}, bf16[1024,256]{1,0:T(8,128)(2,1)S(1)}, u32[]{:S(2)}) copy-start(bf16[1024,256]{1,0:T(8,128)(2,1)S(1)} %get-tuple-element.18) | copy-start | bytes 1572868
  750.0 187.6 %reduce-scatter.15.cloned.1.call-start = ((), (), s32[]{:S(2)}) async-start(), calls=%async_computation.16 | async-start | bytes 20971520 | tf_op jit(solution)/shard_map/reduce_scatter | solution.py:56
  788.3 0.7 copy-start.4
  788.3 149.3 %copy-start.1 = (bf16[4096,256]{1,0:T(8,128)(2,1)S(1)}, bf16[4096,256]{1,0:T(8,128)(2,1)}, u32[]{:S(2)}) copy-start(bf16[4096,256]{1,0:T(8,128)(2,1)} %param.7) | copy-start | bytes 6291460
  788.4 204.5 %all-reduce.5.cloned.1.call-start = ((), (), s32[]{:S(2)}) async-start(), calls=%async_computation.19 | async-start | bytes 1572864 | tf_op jit(solution)/shard_map/psum | solution.py:65
Sparse Core Ops, SparseCore 0:
  48.0 33.2 all-reduce.2
  83.1 81.8 all-gather.8
  195.8 6.4 reduce-scatter.8
  203.7 7.2 all-gather.6
  212.9 7.2 all-gather.10
  242.0 149.1 reduce-scatter.6
  394.2 147.9 reduce-scatter.10
  543.9 81.8 all-gather.12
  628.2 81.8 all-gather.16
  712.1 6.4 reduce-scatter.12
  740.9 6.5 reduce-scatter.16
  750.2 7.2 all-gather.14
  788.5 149.1 reduce-scatter.14
  948.7 44.0 all-reduce.4
where the time goes:
time: 1000 us
  waiting for transfers between devices  665 us (66%)
  matrix products  185 us (18%)
  other arithmetic  128 us (13%)
  between operations  15.8 us (2%)
    reduce_scatter x3, waiting for transfers between devices, device_program(): lax.psum_scatter(user_part, COL_AXES, scatter_dimension=0, tiled=True)  411 us
    all_gather x3, waiting for transfers between devices, device_program(): user_panel = lax.all_gather(user_cur, COL_AXES, axis=0, tiled=True)  152 us
    dot_general x3, matrix products, device_program(): jnp.dot(adjacency, item_panel, preferred_element_type=jnp.float32)  92.8 us
    dot_general x3, matrix products, device_program(): lax.dot_general(adjacency, user_panel, CONTRACT_ROWS, preferred_element_t...  92.1 us
    convert_element_type x1, other arithmetic, build_adjacency(): return weights.astype(jnp.bfloat16)  63.9 us
    psum x1, waiting for transfers between devices, device_program(): loss = bpr_loss(lax.psum(fetched, USER_AXES))  44.2 us
    reduce_sum x1, other arithmetic, device_program(): deg_user = lax.psum(jnp.sum(mask_blk, axis=1), COL_AXES)  40.7 us
    psum x1, waiting for transfers between devices, device_program(): deg_user = lax.psum(jnp.sum(mask_blk, axis=1), COL_AXES)  30.3 us
  transfers between devices with their start and end apart: 14, of which 12 were waited for; matrix products, arithmetic and copies ran while one was open for 20% of the time, Pallas kernels for 0%

commit v1 on v0

v1 whole, which is shorter than its diff:
```python
import functools
import math
import jax
import jax.numpy as jnp
from jax import lax
from jax.experimental import pallas as pl
from jax.experimental.pallas import tpu as pltpu
from jax.sharding import PartitionSpec as P

LAYERS = 3
USER_AXES = ('row', 'cola', 'colb')
ITEM_AXES = ('cola', 'colb', 'row')
COL_AXES = ('cola', 'colb')
F32 = jnp.float32
BF16 = jnp.bfloat16
CONTRACT_ROWS = (((0,), (0,)), ((), ()))
CONTRACT_COLS = (((1,), (1,)), ((), ()))
BUILD = 256
TILE = 512
CHUNK = 32
DEEP = pl.Buffered(4)
OUT = pl.Buffered(2)
LANES = 128


def kernel(dims, mask, user0, item0, triples, user_out, item_out, loss_out, adj, upan, pbuf, precv, sbuf,
           vpan, acc, qrecv, vtot, us, uscol, isc, degu, drecv, degi, degi_recv, sel, selb, selrecv, mine, lsend, lrecv,
           ag_send, ag_recv, rs_send, rs_recv, v_send, v_recv, q_send, q_recv, d_send, d_recv, e_send, e_recv, l_send, l_recv):
    half, items, own_items, dim = dims
    x, y, r = lax.axis_index('colb'), lax.axis_index('cola'), lax.axis_index('row')
    to = {'x': {'colb': 1 - x}, 'y': {'cola': 1 - y}, 'r': {'row': 1 - r},
          'xy': {'colb': 1 - x, 'cola': 1 - y}}
    pending = []
    batch = triples.shape[0]

    def send(src, dst, direction, send_sem, recv_sem):
        copy = pltpu.make_async_remote_copy(src_ref=src, dst_ref=dst, send_sem=send_sem, recv_sem=recv_sem,
                                            device_id=to[direction], device_id_type=pl.DeviceIdType.MESH)
        copy.start()
        pending.append(copy)
        return copy

    def finish(copy):
        copy.wait_send()
        pending[:] = [other for other in pending if other is not copy]

    barrier = pltpu.get_barrier_semaphore()
    for direction in to:
        pl.semaphore_signal(barrier, inc=1, device_id=to[direction], device_id_type=pl.DeviceIdType.MESH)
    pl.semaphore_wait(barrier, 4)

    def own(k, h):
        return user0.at[h] if k == 0 else upan.at[k, 6 + h]

    def gather_start(k):
        return [send(own(k, 0), upan.at[k, 2], 'x', ag_send.at[k, 0], ag_recv.at[k, 0]),
                send(own(k, 1), upan.at[k, 3], 'y', ag_send.at[k, 1], ag_recv.at[k, 1]),
                send(own(k, 0), upan.at[k, 4], 'y', ag_send.at[k, 2], ag_recv.at[k, 2]),
                send(own(k, 1), upan.at[k, 5], 'x', ag_send.at[k, 3], ag_recv.at[k, 3])]

    def gather_forward(k, copies):
        copies[0].wait_recv()
        far0 = send(upan.at[k, 2], upan.at[k, 0], 'y', ag_send.at[k, 4], ag_recv.at[k, 4])
        copies[1].wait_recv()
        far1 = send(upan.at[k, 3], upan.at[k, 1], 'x', ag_send.at[k, 5], ag_recv.at[k, 5])
        return copies[2:] + [far0, far1]

    def wait_all(copies):
        for copy in copies:
            copy.wait_recv()

    gather0 = gather_start(0)
    vpan[0, r] = item0[...]
    item_copy = send(item0, vpan.at[0, r], 'r', v_send.at[0], v_recv.at[0])

    def mask_block(pos, tile):
        h, q = lax.rem(pos, 2), lax.div(pos, 2)
        prim, sec = 1 - lax.div(q, 2), 1 - lax.rem(q, 2)
        dx, dy = prim * (1 - h) + sec * h, sec * (1 - h) + prim * h
        shard = lax.rem(y + dy, 2) * 2 + lax.rem(x + dx, 2)
        return (shard * 2 + h) * (half // BUILD) + tile

    degu[...] = jnp.zeros_like(degu)
    degi[...] = jnp.zeros_like(degi)
    acc[...] = jnp.zeros_like(acc)

    def degree_body(m_ref):
        pos, tile = pl.program_id(0), pl.program_id(1)

        def chunk(i, cols):
            m = m_ref[pl.ds(pl.multiple_of(i * CHUNK, CHUNK), CHUNK), :]
            part = m[:, :LANES]
            for j in range(1, items // LANES):
                part = part + m[:, j * LANES:(j + 1) * LANES]
            uscol[pl.ds(pl.multiple_of(i * CHUNK, CHUNK), CHUNK), :] = part.astype(F32)
            for j in range(CHUNK // 8):
                cols = cols + m[j * 8:(j + 1) * 8, :]
            return cols

        cols = lax.fori_loop(0, BUILD // CHUNK, chunk, jnp.zeros((8, items), jnp.int32))
        degi[...] += cols.astype(F32)
        pick = (lax.broadcasted_iota(jnp.int32, (8, LANES), 0) == tile).astype(BF16)
        degu[pos] += lax.dot_general(pick, uscol[...].astype(BF16), CONTRACT_COLS, preferred_element_type=F32)

    pltpu.emit_pipeline(degree_body, grid=(8, half // BUILD),
                        in_specs=[pl.BlockSpec((BUILD, items), lambda p, t: (mask_block(p, t), 0), pipeline_mode=DEEP)])(mask)
    item_deg = send(degi, degi_recv, 'r', d_send.at[0], d_recv.at[0])
    user_deg = send(degu, drecv.at[0], 'x', d_send.at[1], d_recv.at[1])
    user_deg.wait_recv()
    finish(user_deg)
    for pos in range(8):
        us[pos] = degu[pos] + drecv[0, pos ^ (2 if pos % 2 else 4)]
    user_deg2 = send(us, drecv.at[1], 'y', d_send.at[2], d_recv.at[2])
    rest0 = gather_forward(0, gather0)
    item_deg.wait_recv()
    total = jnp.sum(degi[...] + degi_recv[...], axis=0, keepdims=True)
    isc[...] = lax.rsqrt(jnp.maximum(total, 1.0))
    user_deg2.wait_recv()
    finish(user_deg2)
    for pos in range(8):
        degu[pos] = lax.rsqrt(jnp.maximum(us[pos] + drecv[1, pos ^ (4 if pos % 2 else 2)], 1.0))
    item_copy.wait_recv()

    def panel(k):
        return vpan[k].reshape(items, dim)

    def add_items(a_ref, u_ref):
        for j in range(2):
            acc[j] += lax.dot_general(u_ref[...], a_ref[:, j * own_items:(j + 1) * own_items], CONTRACT_ROWS,
                                      preferred_element_type=F32)

    def build(first, count, users):
        def body(m_ref, *refs):
            (u_ref, a_ref, p_ref) = refs if users is not None else (None,) + refs
            pos, tile = pl.program_id(0) + first, pl.program_id(1)
            row = degu[pos, pl.ds(tile, 1), :]
            uscol[...] = jnp.transpose(jnp.broadcast_to(row, (LANES, BUILD)))

            def chunk(i, carry):
                rows = pl.ds(pl.multiple_of(i * CHUNK, CHUNK), CHUNK)
                scale = uscol[rows, :]
                for j in range(items // LANES):
                    cols = slice(j * LANES, (j + 1) * LANES)
                    weight = (scale * m_ref[rows, cols].astype(F32)) * isc[:, cols]
                    a_ref[rows, cols] = weight.astype(BF16)
                return carry

            lax.fori_loop(0, BUILD // CHUNK, chunk, 0)
            p_ref[...] = jnp.dot(a_ref[...], panel(0), preferred_element_type=F32)
            if users is not None:
                add_items(a_ref, u_ref)

        operands = [mask]
        in_specs = [pl.BlockSpec((BUILD, items), lambda p, t: (mask_block(p + first, t), 0), pipeline_mode=DEEP)]
        if users is not None:
            ref, start = users
            operands.append(ref)
            in_specs.append(pl.BlockSpec((None, BUILD, dim), lambda p, t: (p + (first - start), t, 0), pipeline_mode=DEEP))
        pltpu.emit_pipeline(body, grid=(count, half // BUILD), in_specs=in_specs,
                            out_specs=[pl.BlockSpec((None, BUILD, items), lambda p, t: (p + first, t, 0), pipeline_mode=OUT),
                                       pl.BlockSpec((None, BUILD, dim), lambda p, t: (p + first, t, 0), pipeline_mode=OUT)])(*operands, adj, pbuf.at[0])

    def multiply(k, first, count):
        def body(a_ref, p_ref):
            p_ref[...] = jnp.dot(a_ref[...], panel(k), preferred_element_type=F32)
        pltpu.emit_pipeline(body, grid=(count, half // TILE),
                            in_specs=[pl.BlockSpec((None, TILE, items), lambda p, t: (p + first, t, 0), pipeline_mode=DEEP)],
                            out_specs=[pl.BlockSpec((None, TILE, dim), lambda p, t: (p + first, t, 0), pipeline_mode=OUT)])(adj, pbuf.at[k])

    def accumulate(k, count):
        pltpu.emit_pipeline(add_items, grid=(count, half // TILE),
                            in_specs=[pl.BlockSpec((None, TILE, items), lambda p, t: (p, t, 0), pipeline_mode=DEEP),
                                      pl.BlockSpec((None, TILE, dim), lambda p, t: (p, t, 0), pipeline_mode=DEEP)])(adj, upan.at[k])

    def scatter_send(k, pos):
        return send(pbuf.at[k, pos], precv.at[k, pos], 'y' if pos % 2 else 'x', rs_send.at[k, pos], rs_recv.at[k, pos])

    tile_spec = pl.BlockSpec((TILE, dim), lambda t: (t, 0), pipeline_mode=DEEP)
    out_spec = pl.BlockSpec((TILE, dim), lambda t: (t, 0), pipeline_mode=OUT)

    def scatter_last(k, h, far):
        far.wait_recv()

        def body(p_ref, r_ref, s_ref):
            s_ref[...] = p_ref[...] + r_ref[...]
        pltpu.emit_pipeline(body, grid=(half // TILE,), in_specs=[tile_spec] * 2, out_specs=[out_spec])(
            pbuf.at[k, 4 + h], precv.at[k, h], sbuf.at[k, h])
        return send(sbuf.at[k, h], precv.at[k, 4 + h], 'x' if h else 'y', rs_send.at[k, 4 + h], rs_recv.at[k, 4 + h])

    def scatter_finish(k, h, near, last):
        near.wait_recv()
        last.wait_recv()

        def body(p_ref, n_ref, l_ref, u_ref):
            u_ref[...] = ((p_ref[...] + n_ref[...]) + l_ref[...]).astype(BF16)
        pltpu.emit_pipeline(body, grid=(half // TILE,), in_specs=[tile_spec] * 3, out_specs=[out_spec])(
            pbuf.at[k, 6 + h], precv.at[k, 2 + h], precv.at[k, 4 + h], upan.at[k + 1, 6 + h])

    def item_layer(k):
        copy = send(acc.at[1 - r], qrecv.at[k - 1], 'r', q_send.at[k - 1], q_recv.at[k - 1])
        copy.wait_recv()
        rows = jnp.transpose(acc[r] + qrecv[k - 1]).astype(BF16)
        vtot[...] += rows.astype(F32)
        finish(copy)
        if k < LAYERS:
            vpan[k, r] = rows
            other = send(vpan.at[k, r], vpan.at[k, r], 'r', v_send.at[k], v_recv.at[k])
            acc[...] = jnp.zeros_like(acc)
            other.wait_recv()

    vtot[...] = item0[...].astype(F32)
    far, near = {}, {}
    build(0, 1, None)
    far[0, 0] = scatter_send(0, 0)
    build(1, 1, None)
    far[0, 1] = scatter_send(0, 1)
    build(2, 1, (upan.at[0], 0))
    near[0, 0] = scatter_send(0, 2)
    build(3, 1, (upan.at[0], 0))
    near[0, 1] = scatter_send(0, 3)
    wait_all(rest0[:2])
    build(4, 2, (upan.at[0], 0))
    build(6, 2, (user0, 6))
    wait_all(rest0[2:])
    last0 = [scatter_last(0, h, far[0, h]) for h in (0, 1)]
    accumulate(0, 2)
    item_layer(1)
    for pos in range(2):
        multiply(1, pos, 1)
        far[1, pos] = scatter_send(1, pos)
    multiply(1, 2, 6)
    for h in (0, 1):
        scatter_finish(0, h, near[0, h], last0[h])
    gather1 = gather_start(1)
    rest1 = gather_forward(1, gather1)
    for pos in (2, 3):
        near[1, pos % 2] = scatter_send(1, pos)
    last1 = [scatter_last(1, h, far[1, h]) for h in (0, 1)]
    wait_all(rest1)
    accumulate(1, 8)
    item_layer(2)
    for pos in range(2):
        multiply(2, pos, 1)
        far[2, pos] = scatter_send(2, pos)
    multiply(2, 2, 6)
    for h in (0, 1):
        scatter_finish(1, h, near[1, h], last1[h])
    gather2 = gather_start(2)
    rest2 = gather_forward(2, gather2)
    last2 = [scatter_last(2, h, far[2, h]) for h in (0, 1)]
    wait_all(rest2)
    accumulate(2, 8)
    item_layer(3)

    out_rows = (vtot[...] / (LAYERS + 1)).astype(BF16)
    item_out[...] = out_rows
    item_base = ((y * 2 + x) * 2 + r) * own_items
    for j in range(2):
        hit = (triples[:, 1 + j:2 + j] - item_base) == lax.broadcasted_iota(jnp.int32, (batch, own_items), 1)
        selb[j] = jnp.dot(hit.astype(BF16), out_rows, preferred_element_type=F32).astype(BF16)
    core = send(selb.at[1 - r], selrecv.at[0], 'r', e_send.at[0], e_recv.at[0])
    core.wait_recv()
    sel[...] = selb[r] + selrecv[0]
    shared = [send(sel, selrecv.at[i], direction, e_send.at[i], e_recv.at[i]) for i, direction in ((1, 'x'), (2, 'y'), (3, 'xy'))]
    for pos in (2, 3):
        near[2, pos % 2] = scatter_send(2, pos)
    wait_all(shared)
    finish(core)
    selb[r] = (sel[...] + selrecv[1]) + (selrecv[2] + selrecv[3])
    back = send(selb.at[r], selrecv.at[4], 'r', e_send.at[4], e_recv.at[4])
    back.wait_recv()

    user_base = ((r * 2 + y) * 2 + x) * (2 * half)
    mine[...] = jnp.zeros_like(mine)
    for h in (0, 1):
        near[2, h].wait_recv()
        last2[h].wait_recv()

        def body(p_ref, n_ref, l_ref, u0_ref, u1_ref, u2_ref, o_ref, h=h):
            last_user = ((p_ref[...] + n_ref[...]) + l_ref[...]).astype(BF16)
            rows = u0_ref[...].astype(F32) + u1_ref[...].astype(F32)
            rows = (rows + u2_ref[...].astype(F32)) + last_user.astype(F32)
            rows = (rows / (LAYERS + 1)).astype(BF16)
            o_ref[...] = rows
            first = user_base + h * half + pl.program_id(0) * TILE
            hit = (triples[:, 0:1] - first) == lax.broadcasted_iota(jnp.int32, (batch, TILE), 1)
            mine[...] += jnp.dot(hit.astype(BF16), rows, preferred_element_type=F32)
        pltpu.emit_pipeline(body, grid=(half // TILE,), in_specs=[tile_spec] * 6, out_specs=[out_spec])(
            pbuf.at[2, 6 + h], precv.at[2, 2 + h], precv.at[2, 4 + h], user0.at[h], upan.at[1, 6 + h], upan.at[2, 6 + h],
            user_out.at[h])
    own_rows, other_rows = selb[r].astype(F32), selrecv[4].astype(F32)
    pos_rows = jnp.where(r == 0, own_rows, other_rows)
    neg_rows = jnp.where(r == 0, other_rows, own_rows)
    rows = mine[...]
    margin = (jnp.sum(rows * pos_rows, axis=1, keepdims=True) - jnp.sum(rows * neg_rows, axis=1, keepdims=True)) / math.sqrt(dim)
    local = triples[:, 0:1] - user_base
    soft = jnp.maximum(-margin, 0.0) + jnp.log1p(jnp.exp(-jnp.abs(margin)))
    terms = jnp.where((local >= 0) & (local < 2 * half), soft, 0.0)
    value = jnp.broadcast_to(jnp.sum(terms, axis=0, keepdims=True), (8, LANES))
    for i, direction in enumerate('rxy'):
        lsend[i] = value
        send(lsend.at[i], lrecv.at[i], direction, l_send.at[i], l_recv.at[i]).wait_recv()
        value = value + lrecv[i]
    loss_out[...] = value[0:1, 0:1] / batch
    for copy in pending:
        copy.wait_send()


def solution(mesh):
    def device_program(mask_blk, user_shard, item_shard, triples):
        shard, dim = user_shard.shape
        half, items, own_items, batch = shard // 2, mask_blk.shape[1], item_shard.shape[0], triples.shape[0]
        hbm = pl.BlockSpec(memory_space=pl.ANY)
        vmem = pl.BlockSpec(memory_space=pltpu.VMEM)
        shapes = [((2, half, dim), BF16), ((own_items, dim), BF16), ((1, 1), F32), ((8, half, items), BF16),
                  ((LAYERS, 8, half, dim), BF16), ((LAYERS, 8, half, dim), F32), ((LAYERS, 6, half, dim), F32),
                  ((LAYERS, 2, half, dim), F32)]
        dma = pltpu.SemaphoreType.DMA
        outs = pl.pallas_call(
            functools.partial(kernel, (half, items, own_items, dim)),
            out_shape=[jax.ShapeDtypeStruct(*shape) for shape in shapes],
            in_specs=[hbm, hbm, vmem, vmem],
            out_specs=[hbm, vmem, vmem] + [hbm] * 5,
            scratch_shapes=[
                pltpu.VMEM((LAYERS, 2, own_items, dim), BF16), pltpu.VMEM((2, dim, own_items), F32),
                pltpu.VMEM((LAYERS, dim, own_items), F32), pltpu.VMEM((own_items, dim), F32),
                pltpu.VMEM((8, 8, BUILD), F32), pltpu.VMEM((BUILD, LANES), F32), pltpu.VMEM((1, items), F32),
                pltpu.VMEM((8, 8, BUILD), F32), pltpu.VMEM((2, 8, 8, BUILD), F32),
                pltpu.VMEM((8, items), F32), pltpu.VMEM((8, items), F32),
                pltpu.VMEM((batch, dim), BF16), pltpu.VMEM((2, batch, dim), BF16), pltpu.VMEM((5, batch, dim), BF16),
                pltpu.VMEM((batch, dim), F32), pltpu.VMEM((3, 8, LANES), F32), pltpu.VMEM((3, 8, LANES), F32),
                dma((LAYERS, 6)), dma((LAYERS, 6)), dma((LAYERS, 6)), dma((LAYERS, 6)), dma((LAYERS,)), dma((LAYERS,)),
                dma((LAYERS,)), dma((LAYERS,)), dma((3,)), dma((3,)), dma((5,)), dma((5,)), dma((3,)), dma((3,))],
            compiler_params=pltpu.CompilerParams(collective_id=0, has_side_effects=True, vmem_limit_bytes=60 * 1024 * 1024),
        )(mask_blk, user_shard.reshape(2, half, dim), item_shard, triples)
        return outs[0].reshape(shard, dim), outs[1], outs[2].reshape(())

    return jax.shard_map(device_program, mesh=mesh, in_specs=(P('row', COL_AXES), P(USER_AXES, None), P(ITEM_AXES, None), P()), out_specs=(P(USER_AXES, None), P(ITEM_AXES, None), P()), check_vma=False)
```

time: 1000 us -> 648 us (0.65)
  waiting for transfers between devices: 665 us -> 0 us
  Pallas kernels: 0 us -> 639 us
  matrix products: 185 us -> 0 us
  other arithmetic: 128 us -> 0 us
  between operations: 15.8 us -> 2.4 us
    pallas_call x0 -> x1, Pallas kernels: none -> 639 us  [device_program(): pl.pallas_call(functools.partial(kernel, (half, items, own_items, dim)),...]
    reduce_scatter x6 -> x0, waiting for transfers between devices: 424 us -> none  [the longest x3 411 us: device_program(): lax.psum_scatter(user_part, COL_AXES, scatter_dimension=0, tiled=True)]
    dot_general x6 -> x0, matrix products: 185 us -> none  [the longest x3 92.8 us: device_program(): jnp.dot(adjacency, item_panel, preferred_element_type=jnp.float32)]
    all_gather x6 -> x0, waiting for transfers between devices: 166 us -> none  [the longest x3 152 us: device_program(): user_panel = lax.all_gather(user_cur, COL_AXES, axis=0, tiled=True)]
    convert_element_type x6 -> x0, other arithmetic: 83 us -> none  [the longest x1 63.9 us: build_adjacency(): return weights.astype(jnp.bfloat16)]
    psum x2 -> x0, waiting for transfers between devices: 74.5 us -> none  [the longest x1 44.2 us: device_program(): loss = bpr_loss(lax.psum(fetched, USER_AXES))]
    reduce_sum x3 -> x0, other arithmetic: 42.6 us -> none  [the longest x1 40.7 us: device_program(): deg_user = lax.psum(jnp.sum(mask_blk, axis=1), COL_AXES)]
  transfers between devices with their start and end apart: 14 -> 0, of which waited for: 12 -> 0; matrix products, arithmetic and copies ran while one was open for 20% -> 0% of each run, Pallas kernels for 0% -> 0%
where the time goes in v1:
time: 648 us; the launch traced here: 647 us
  Pallas kernels  639 us (99%)
    pallas_call x1, Pallas kernels, device_program(): pl.pallas_call(functools.partial(kernel, (half, items, own_items, dim)),...  639 us

profile of v1, /device:TPU:0, one launch (start us, length us, event | category | flops | bytes accessed | tf_op | source)
XLA Modules:
  0.0 647.4 jit_solution(2547000941289214790)
XLA Ops:
  0.6 1.5 copy.7.triples
  2.1 638.6 %shard_map.67 = (bf16[2,2048,256]{2,1,0:T(8,128)(2,1)}, bf16[1024,256]{1,0:T(8,128)(2,1)}, f32[1,1]{1,0:T(1,128)}, bf16[8,2048,2048]{2,1,0:T(8,128)(2,1)}, bf16[...) custom-call(s32[16384,2048]{1,0:T(8,128)} %mask.1, ...), custom_call_target="tpu_custom_call" | custom-call | tf_op jit(solution)/shard_map/pallas_call | solution.py:319
  640.7 3.0 copy.11
  643.7 1.9 copy.12

commit v2 on v1

--- a/solution.py
+++ b/solution.py
@@ -1,4 +1,5 @@
 import functools
+import itertools
 import math
 import jax
 import jax.numpy as jnp
@@ -18,6 +19,7 @@
 BUILD = 256
 TILE = 512
 CHUNK = 32
+PARTS = 4
 DEEP = pl.Buffered(4)
 OUT = pl.Buffered(2)
 LANES = 128
@@ -25,29 +27,38 @@
 
 def kernel(dims, mask, user0, item0, triples, user_out, item_out, loss_out, adj, upan, pbuf, precv, sbuf,
            vpan, acc, qrecv, vtot, us, uscol, isc, degu, drecv, degi, degi_recv, sel, selb, selrecv, mine, lsend, lrecv,
+           ids, idcol, base, usum, nearv, outv, iout, local_sem, out_sem,
            ag_send, ag_recv, rs_send, rs_recv, v_send, v_recv, q_send, q_recv, d_send, d_recv, e_send, e_recv, l_send, l_recv):
     half, items, own_items, dim = dims
     x, y, r = lax.axis_index('colb'), lax.axis_index('cola'), lax.axis_index('row')
-    to = {'x': {'colb': 1 - x}, 'y': {'cola': 1 - y}, 'r': {'row': 1 - r},
-          'xy': {'colb': 1 - x, 'cola': 1 - y}}
+    to = {'x': {'colb': 1 - x}, 'y': {'cola': 1 - y}, 'r': {'row': 1 - r}}
+    others = [{'cola': 1 - y if dy else y, 'colb': 1 - x if dx else x, 'row': 1 - r if dr else r}
+              for dy, dx, dr in itertools.product((0, 1), repeat=3) if dy or dx or dr]
     pending = []
-    batch = triples.shape[0]
-
-    def send(src, dst, direction, send_sem, recv_sem):
+    batch = ids.shape[1]
+
+    def send_to(src, dst, device, send_sem, recv_sem):
         copy = pltpu.make_async_remote_copy(src_ref=src, dst_ref=dst, send_sem=send_sem, recv_sem=recv_sem,
-                                            device_id=to[direction], device_id_type=pl.DeviceIdType.MESH)
+                                            device_id=device, device_id_type=pl.DeviceIdType.MESH)
         copy.start()
         pending.append(copy)
         return copy
 
+    def send(src, dst, direction, send_sem, recv_sem):
+        return send_to(src, dst, to[direction], send_sem, recv_sem)
+
     def finish(copy):
         copy.wait_send()
         pending[:] = [other for other in pending if other is not copy]
 
+    item_in = pltpu.make_async_copy(item0, vpan.at[0, r], local_sem.at[0])
+    ids_in = pltpu.make_async_copy(triples, ids, local_sem.at[1])
+    item_in.start()
+    ids_in.start()
     barrier = pltpu.get_barrier_semaphore()
-    for direction in to:
-        pl.semaphore_signal(barrier, inc=1, device_id=to[direction], device_id_type=pl.DeviceIdType.MESH)
-    pl.semaphore_wait(barrier, 4)
+    for device in others:
+        pl.semaphore_signal(barrier, inc=1, device_id=device, device_id_type=pl.DeviceIdType.MESH)
+    pl.semaphore_wait(barrier, len(others))
 
     def own(k, h):
         return user0.at[h] if k == 0 else upan.at[k, 6 + h]
@@ -70,7 +81,8 @@
             copy.wait_recv()
 
     gather0 = gather_start(0)
-    vpan[0, r] = item0[...]
+    item_in.wait()
+    ids_in.wait()
     item_copy = send(item0, vpan.at[0, r], 'r', v_send.at[0], v_recv.at[0])
 
     def mask_block(pos, tile):
@@ -129,10 +141,10 @@
             acc[j] += lax.dot_general(u_ref[...], a_ref[:, j * own_items:(j + 1) * own_items], CONTRACT_ROWS,
                                       preferred_element_type=F32)
 
-    def build(first, count, users):
+    def build(first, count, users, start_tile=0, tiles=half // BUILD):
         def body(m_ref, *refs):
             (u_ref, a_ref, p_ref) = refs if users is not None else (None,) + refs
-            pos, tile = pl.program_id(0) + first, pl.program_id(1)
+            pos, tile = pl.program_id(0) + first, pl.program_id(1) + start_tile
             row = degu[pos, pl.ds(tile, 1), :]
             uscol[...] = jnp.transpose(jnp.broadcast_to(row, (LANES, BUILD)))
 
@@ -151,14 +163,14 @@
                 add_items(a_ref, u_ref)
 
         operands = [mask]
-        in_specs = [pl.BlockSpec((BUILD, items), lambda p, t: (mask_block(p + first, t), 0), pipeline_mode=DEEP)]
+        in_specs = [pl.BlockSpec((BUILD, items), lambda p, t: (mask_block(p + first, t + start_tile), 0), pipeline_mode=DEEP)]
         if users is not None:
             ref, start = users
             operands.append(ref)
-            in_specs.append(pl.BlockSpec((None, BUILD, dim), lambda p, t: (p + (first - start), t, 0), pipeline_mode=DEEP))
-        pltpu.emit_pipeline(body, grid=(count, half // BUILD), in_specs=in_specs,
-                            out_specs=[pl.BlockSpec((None, BUILD, items), lambda p, t: (p + first, t, 0), pipeline_mode=OUT),
-                                       pl.BlockSpec((None, BUILD, dim), lambda p, t: (p + first, t, 0), pipeline_mode=OUT)])(*operands, adj, pbuf.at[0])
+            in_specs.append(pl.BlockSpec((None, BUILD, dim), lambda p, t: (p + (first - start), t + start_tile, 0), pipeline_mode=DEEP))
+        pltpu.emit_pipeline(body, grid=(count, tiles), in_specs=in_specs,
+                            out_specs=[pl.BlockSpec((None, BUILD, items), lambda p, t: (p + first, t + start_tile, 0), pipeline_mode=OUT),
+                                       pl.BlockSpec((None, BUILD, dim), lambda p, t: (p + first, t + start_tile, 0), pipeline_mode=OUT)])(*operands, adj, pbuf.at[0])
 
     def multiply(k, first, count):
         def body(a_ref, p_ref):
@@ -172,20 +184,22 @@
                             in_specs=[pl.BlockSpec((None, TILE, items), lambda p, t: (p, t, 0), pipeline_mode=DEEP),
                                       pl.BlockSpec((None, TILE, dim), lambda p, t: (p, t, 0), pipeline_mode=DEEP)])(adj, upan.at[k])
 
-    def scatter_send(k, pos):
-        return send(pbuf.at[k, pos], precv.at[k, pos], 'y' if pos % 2 else 'x', rs_send.at[k, pos], rs_recv.at[k, pos])
+    def scatter_send(k, pos, part=0, parts=1):
+        rows = pl.ds(part * (half // parts), half // parts)
+        dst = nearv.at[pos - 2, rows] if k == LAYERS - 1 and pos >= 2 else precv.at[k, pos, rows]
+        return send(pbuf.at[k, pos, rows], dst, 'y' if pos % 2 else 'x', rs_send.at[k, pos, part], rs_recv.at[k, pos, part])
 
     tile_spec = pl.BlockSpec((TILE, dim), lambda t: (t, 0), pipeline_mode=DEEP)
     out_spec = pl.BlockSpec((TILE, dim), lambda t: (t, 0), pipeline_mode=OUT)
 
     def scatter_last(k, h, far):
-        far.wait_recv()
+        wait_all(far)
 
         def body(p_ref, r_ref, s_ref):
             s_ref[...] = p_ref[...] + r_ref[...]
         pltpu.emit_pipeline(body, grid=(half // TILE,), in_specs=[tile_spec] * 2, out_specs=[out_spec])(
             pbuf.at[k, 4 + h], precv.at[k, h], sbuf.at[k, h])
-        return send(sbuf.at[k, h], precv.at[k, 4 + h], 'x' if h else 'y', rs_send.at[k, 4 + h], rs_recv.at[k, 4 + h])
+        return send(sbuf.at[k, h], precv.at[k, 4 + h], 'x' if h else 'y', rs_send.at[k, 4 + h, 0], rs_recv.at[k, 4 + h, 0])
 
     def scatter_finish(k, h, near, last):
         near.wait_recv()
@@ -208,12 +222,17 @@
             acc[...] = jnp.zeros_like(acc)
             other.wait_recv()
 
-    vtot[...] = item0[...].astype(F32)
+    vtot[...] = vpan[0, r].astype(F32)
+    for j in range(3):
+        row = jnp.broadcast_to(ids[j:j + 1, :].astype(F32), (LANES, batch))
+        idcol[j] = jnp.transpose(row).astype(jnp.int32)
     far, near = {}, {}
     build(0, 1, None)
-    far[0, 0] = scatter_send(0, 0)
-    build(1, 1, None)
-    far[0, 1] = scatter_send(0, 1)
+    far[0, 0] = [scatter_send(0, 0)]
+    far[0, 1] = []
+    for part in range(2):
+        build(1, 1, None, part * (half // BUILD // 2), half // BUILD // 2)
+        far[0, 1].append(scatter_send(0, 1, part, 2))
     build(2, 1, (upan.at[0], 0))
     near[0, 0] = scatter_send(0, 2)
     build(3, 1, (upan.at[0], 0))
@@ -227,7 +246,7 @@
     item_layer(1)
     for pos in range(2):
         multiply(1, pos, 1)
-        far[1, pos] = scatter_send(1, pos)
+        far[1, pos] = [scatter_send(1, pos)]
     multiply(1, 2, 6)
     for h in (0, 1):
         scatter_finish(0, h, near[0, h], last0[h])
@@ -241,7 +260,7 @@
     item_layer(2)
     for pos in range(2):
         multiply(2, pos, 1)
-        far[2, pos] = scatter_send(2, pos)
+        far[2, pos] = [scatter_send(2, pos)]
     multiply(2, 2, 6)
     for h in (0, 1):
         scatter_finish(1, h, near[1, h], last1[h])
@@ -253,57 +272,76 @@
     item_layer(3)
 
     out_rows = (vtot[...] / (LAYERS + 1)).astype(BF16)
-    item_out[...] = out_rows
+    iout[...] = out_rows
+    item_done = pltpu.make_async_copy(iout, item_out, local_sem.at[2])
+    item_done.start()
     item_base = ((y * 2 + x) * 2 + r) * own_items
     for j in range(2):
-        hit = (triples[:, 1 + j:2 + j] - item_base) == lax.broadcasted_iota(jnp.int32, (batch, own_items), 1)
+        hit = (idcol[1 + j, :, 0:1] - item_base) == lax.broadcasted_iota(jnp.int32, (batch, own_items), 1)
         selb[j] = jnp.dot(hit.astype(BF16), out_rows, preferred_element_type=F32).astype(BF16)
     core = send(selb.at[1 - r], selrecv.at[0], 'r', e_send.at[0], e_recv.at[0])
     core.wait_recv()
-    sel[...] = selb[r] + selrecv[0]
-    shared = [send(sel, selrecv.at[i], direction, e_send.at[i], e_recv.at[i]) for i, direction in ((1, 'x'), (2, 'y'), (3, 'xy'))]
-    for pos in (2, 3):
-        near[2, pos % 2] = scatter_send(2, pos)
-    wait_all(shared)
+    sel[0] = selb[r] + selrecv[0]
+    xrow = send(sel.at[0], selrecv.at[1], 'x', e_send.at[1], e_recv.at[1])
+    parts = {2: [scatter_send(2, 2, 0, PARTS)], 3: [scatter_send(2, 3, 0, PARTS)]}
+    xrow.wait_recv()
+    sel[1] = sel[0] + selrecv[1]
+    yrow = send(sel.at[1], selrecv.at[2], 'y', e_send.at[2], e_recv.at[2])
+    for part in range(1, PARTS):
+        for pos in (2, 3):
+            parts[pos].append(scatter_send(2, pos, part, PARTS))
+
+    for h in (0, 1):
+        last2[h].wait_recv()
+
+        def body(p_ref, l_ref, u0_ref, u1_ref, u2_ref, h=h):
+            rows = pl.ds(pl.multiple_of(pl.program_id(0) * TILE, TILE), TILE)
+            base[h, rows, :] = p_ref[...] + l_ref[...]
+            usum[h, rows, :] = (u0_ref[...].astype(F32) + u1_ref[...].astype(F32)) + u2_ref[...].astype(F32)
+        pltpu.emit_pipeline(body, grid=(half // TILE,), in_specs=[tile_spec] * 5)(
+            pbuf.at[2, 6 + h], precv.at[2, 4 + h], user0.at[h], upan.at[1, 6 + h], upan.at[2, 6 + h])
+    yrow.wait_recv()
     finish(core)
-    selb[r] = (sel[...] + selrecv[1]) + (selrecv[2] + selrecv[3])
-    back = send(selb.at[r], selrecv.at[4], 'r', e_send.at[4], e_recv.at[4])
+    selb[r] = sel[1] + selrecv[2]
+    back = send(selb.at[r], selrecv.at[3], 'r', e_send.at[3], e_recv.at[3])
     back.wait_recv()
 
     user_base = ((r * 2 + y) * 2 + x) * (2 * half)
+    local = idcol[0, :, 0:1] - user_base
     mine[...] = jnp.zeros_like(mine)
-    for h in (0, 1):
-        near[2, h].wait_recv()
-        last2[h].wait_recv()
-
-        def body(p_ref, n_ref, l_ref, u0_ref, u1_ref, u2_ref, o_ref, h=h):
-            last_user = ((p_ref[...] + n_ref[...]) + l_ref[...]).astype(BF16)
-            rows = u0_ref[...].astype(F32) + u1_ref[...].astype(F32)
-            rows = (rows + u2_ref[...].astype(F32)) + last_user.astype(F32)
-            rows = (rows / (LAYERS + 1)).astype(BF16)
-            o_ref[...] = rows
-            first = user_base + h * half + pl.program_id(0) * TILE
-            hit = (triples[:, 0:1] - first) == lax.broadcasted_iota(jnp.int32, (batch, TILE), 1)
-            mine[...] += jnp.dot(hit.astype(BF16), rows, preferred_element_type=F32)
-        pltpu.emit_pipeline(body, grid=(half // TILE,), in_specs=[tile_spec] * 6, out_specs=[out_spec])(
-            pbuf.at[2, 6 + h], precv.at[2, 2 + h], precv.at[2, 4 + h], user0.at[h], upan.at[1, 6 + h], upan.at[2, 6 + h],
-            user_out.at[h])
-    own_rows, other_rows = selb[r].astype(F32), selrecv[4].astype(F32)
+    size = half // PARTS
+    stores = []
+    for part in range(PARTS):
+        rows = pl.ds(part * size, size)
+        for h in (0, 1):
+            parts[2 + h][part].wait_recv()
+            last_user = (base[h, rows, :] + nearv[h, rows, :]).astype(BF16)
+            mean = ((usum[h, rows, :] + last_user.astype(F32)) / (LAYERS + 1)).astype(BF16)
+            outv[h, rows, :] = mean
+            store = pltpu.make_async_copy(outv.at[h, rows], user_out.at[h, rows], out_sem.at[h, part])
+            store.start()
+            stores.append(store)
+            hit = (local - (h * half + part * size)) == lax.broadcasted_iota(jnp.int32, (batch, size), 1)
+            mine[...] += jnp.dot(hit.astype(BF16), mean, preferred_element_type=F32)
+    own_rows, other_rows = selb[r].astype(F32), selrecv[3].astype(F32)
     pos_rows = jnp.where(r == 0, own_rows, other_rows)
     neg_rows = jnp.where(r == 0, other_rows, own_rows)
     rows = mine[...]
     margin = (jnp.sum(rows * pos_rows, axis=1, keepdims=True) - jnp.sum(rows * neg_rows, axis=1, keepdims=True)) / math.sqrt(dim)
-    local = triples[:, 0:1] - user_base
     soft = jnp.maximum(-margin, 0.0) + jnp.log1p(jnp.exp(-jnp.abs(margin)))
     terms = jnp.where((local >= 0) & (local < 2 * half), soft, 0.0)
-    value = jnp.broadcast_to(jnp.sum(terms, axis=0, keepdims=True), (8, LANES))
-    for i, direction in enumerate('rxy'):
-        lsend[i] = value
-        send(lsend.at[i], lrecv.at[i], direction, l_send.at[i], l_recv.at[i]).wait_recv()
-        value = value + lrecv[i]
-    loss_out[...] = value[0:1, 0:1] / batch
+    lsend[...] = jnp.broadcast_to(jnp.sum(terms, axis=0, keepdims=True), (8, LANES))
+    shared = [send_to(lsend, lrecv.at[i], device, l_send.at[i], l_recv.at[i]) for i, device in enumerate(others)]
+    for store in stores:
+        store.wait()
+    item_done.wait()
     for copy in pending:
         copy.wait_send()
+    wait_all(shared)
+    level = [lsend[...]] + [lrecv[i] for i in range(len(others))]
+    while len(level) > 1:
+        level = [level[i] + level[i + 1] for i in range(0, len(level), 2)]
+    loss_out[...] = level[0][0:1, 0:1] / batch
 
 
 def solution(mesh):
@@ -319,20 +357,23 @@
         outs = pl.pallas_call(
             functools.partial(kernel, (half, items, own_items, dim)),
             out_shape=[jax.ShapeDtypeStruct(*shape) for shape in shapes],
-            in_specs=[hbm, hbm, vmem, vmem],
-            out_specs=[hbm, vmem, vmem] + [hbm] * 5,
+            in_specs=[hbm] * 4,
+            out_specs=[hbm, hbm, vmem] + [hbm] * 5,
             scratch_shapes=[
                 pltpu.VMEM((LAYERS, 2, own_items, dim), BF16), pltpu.VMEM((2, dim, own_items), F32),
                 pltpu.VMEM((LAYERS, dim, own_items), F32), pltpu.VMEM((own_items, dim), F32),
                 pltpu.VMEM((8, 8, BUILD), F32), pltpu.VMEM((BUILD, LANES), F32), pltpu.VMEM((1, items), F32),
                 pltpu.VMEM((8, 8, BUILD), F32), pltpu.VMEM((2, 8, 8, BUILD), F32),
                 pltpu.VMEM((8, items), F32), pltpu.VMEM((8, items), F32),
-                pltpu.VMEM((batch, dim), BF16), pltpu.VMEM((2, batch, dim), BF16), pltpu.VMEM((5, batch, dim), BF16),
-                pltpu.VMEM((batch, dim), F32), pltpu.VMEM((3, 8, LANES), F32), pltpu.VMEM((3, 8, LANES), F32),
-                dma((LAYERS, 6)), dma((LAYERS, 6)), dma((LAYERS, 6)), dma((LAYERS, 6)), dma((LAYERS,)), dma((LAYERS,)),
-                dma((LAYERS,)), dma((LAYERS,)), dma((3,)), dma((3,)), dma((5,)), dma((5,)), dma((3,)), dma((3,))],
+                pltpu.VMEM((2, batch, dim), BF16), pltpu.VMEM((2, batch, dim), BF16), pltpu.VMEM((4, batch, dim), BF16),
+                pltpu.VMEM((batch, dim), F32), pltpu.VMEM((8, LANES), F32), pltpu.VMEM((7, 8, LANES), F32),
+                pltpu.VMEM((3, batch), jnp.int32), pltpu.VMEM((3, batch, LANES), jnp.int32),
+                pltpu.VMEM((2, half, dim), F32), pltpu.VMEM((2, half, dim), F32), pltpu.VMEM((2, half, dim), F32),
+                pltpu.VMEM((2, half, dim), BF16), pltpu.VMEM((own_items, dim), BF16), dma((3,)), dma((2, PARTS)),
+                dma((LAYERS, 6)), dma((LAYERS, 6)), dma((LAYERS, 6, PARTS)), dma((LAYERS, 6, PARTS)), dma((LAYERS,)), dma((LAYERS,)),
+                dma((LAYERS,)), dma((LAYERS,)), dma((3,)), dma((3,)), dma((4,)), dma((4,)), dma((7,)), dma((7,))],
             compiler_params=pltpu.CompilerParams(collective_id=0, has_side_effects=True, vmem_limit_bytes=60 * 1024 * 1024),
-        )(mask_blk, user_shard.reshape(2, half, dim), item_shard, triples)
+        )(mask_blk, user_shard.reshape(2, half, dim), item_shard, triples.T)
         return outs[0].reshape(shard, dim), outs[1], outs[2].reshape(())
 
     return jax.shard_map(device_program, mesh=mesh, in_specs=(P('row', COL_AXES), P(USER_AXES, None), P(ITEM_AXES, None), P()), out_specs=(P(USER_AXES, None), P(ITEM_AXES, None), P()), check_vma=False)

time: 648 us -> 634 us (0.978)
  Pallas kernels: 639 us -> 626 us
    pallas_call x1, Pallas kernels: 639 us -> 626 us  [device_program(): pl.pallas_call(functools.partial(kernel, (half, items, own_items, dim)),...]
where the time goes in v2:
time: 634 us
  Pallas kernels  626 us (99%)
    pallas_call x1, Pallas kernels, device_program(): pl.pallas_call(functools.partial(kernel, (half, items, own_items, dim)),...  626 us

profile of v2, /device:TPU:0, one launch (start us, length us, event | category | flops | bytes accessed | tf_op | source)
XLA Modules:
  0.0 633.7 jit_solution(7207233875870350166)
XLA Ops:
  0.6 626.4 %shard_map.67 = (bf16[2,2048,256]{2,1,0:T(8,128)(2,1)}, bf16[1024,256]{1,0:T(8,128)(2,1)}, f32[1,1]{1,0:T(1,128)}, bf16[8,2048,2048]{2,1,0:T(8,128)(2,1)}, bf16[...) custom-call(s32[16384,2048]{1,0:T(8,128)} %mask.1, ...), custom_call_target="tpu_custom_call" | custom-call | tf_op jit(solution)/shard_map/pallas_call | solution.py:357
  627.0 3.0 copy.10
  630.0 1.9 copy.11

commit v3 on v2

--- a/solution.py
+++ b/solution.py
@@ -27,11 +27,12 @@
 
 def kernel(dims, mask, user0, item0, triples, user_out, item_out, loss_out, adj, upan, pbuf, precv, sbuf,
            vpan, acc, qrecv, vtot, us, uscol, isc, degu, drecv, degi, degi_recv, sel, selb, selrecv, mine, lsend, lrecv,
-           ids, idcol, base, usum, nearv, outv, iout, local_sem, out_sem,
-           ag_send, ag_recv, rs_send, rs_recv, v_send, v_recv, q_send, q_recv, d_send, d_recv, e_send, e_recv, l_send, l_recv):
+           ids, idcol, base, usum, nearv, local_sem,
+           ag_send, ag_recv, rs_send, rs_recv, p_send, p_recv, v_send, v_recv, q_send, q_recv, d_send, d_recv, e_send, e_recv, l_send, l_recv):
     half, items, own_items, dim = dims
     x, y, r = lax.axis_index('colb'), lax.axis_index('cola'), lax.axis_index('row')
-    to = {'x': {'colb': 1 - x}, 'y': {'cola': 1 - y}, 'r': {'row': 1 - r}}
+    to = {'x': {'colb': 1 - x}, 'y': {'cola': 1 - y}, 'r': {'row': 1 - r},
+          'xy': {'colb': 1 - x, 'cola': 1 - y}}
     others = [{'cola': 1 - y if dy else y, 'colb': 1 - x if dx else x, 'row': 1 - r if dr else r}
               for dy, dx, dr in itertools.product((0, 1), repeat=3) if dy or dx or dr]
     pending = []
@@ -117,20 +118,16 @@
     pltpu.emit_pipeline(degree_body, grid=(8, half // BUILD),
                         in_specs=[pl.BlockSpec((BUILD, items), lambda p, t: (mask_block(p, t), 0), pipeline_mode=DEEP)])(mask)
     item_deg = send(degi, degi_recv, 'r', d_send.at[0], d_recv.at[0])
-    user_deg = send(degu, drecv.at[0], 'x', d_send.at[1], d_recv.at[1])
-    user_deg.wait_recv()
-    finish(user_deg)
-    for pos in range(8):
-        us[pos] = degu[pos] + drecv[0, pos ^ (2 if pos % 2 else 4)]
-    user_deg2 = send(us, drecv.at[1], 'y', d_send.at[2], d_recv.at[2])
+    user_deg = [send(degu, drecv.at[i], direction, d_send.at[1 + i], d_recv.at[1 + i]) for i, direction in enumerate(('x', 'y', 'xy'))]
     rest0 = gather_forward(0, gather0)
     item_deg.wait_recv()
     total = jnp.sum(degi[...] + degi_recv[...], axis=0, keepdims=True)
     isc[...] = lax.rsqrt(jnp.maximum(total, 1.0))
-    user_deg2.wait_recv()
-    finish(user_deg2)
+    wait_all(user_deg)
     for pos in range(8):
-        degu[pos] = lax.rsqrt(jnp.maximum(us[pos] + drecv[1, pos ^ (4 if pos % 2 else 2)], 1.0))
+        flips = (2, 4, 6) if pos % 2 else (4, 2, 6)
+        count = (degu[pos] + drecv[0, pos ^ flips[0]]) + (drecv[1, pos ^ flips[1]] + drecv[2, pos ^ flips[2]])
+        us[pos] = lax.rsqrt(jnp.maximum(count, 1.0))
     item_copy.wait_recv()
 
     def panel(k):
@@ -145,7 +142,7 @@
         def body(m_ref, *refs):
             (u_ref, a_ref, p_ref) = refs if users is not None else (None,) + refs
             pos, tile = pl.program_id(0) + first, pl.program_id(1) + start_tile
-            row = degu[pos, pl.ds(tile, 1), :]
+            row = us[pos, pl.ds(tile, 1), :]
             uscol[...] = jnp.transpose(jnp.broadcast_to(row, (LANES, BUILD)))
 
             def chunk(i, carry):
@@ -186,8 +183,11 @@
 
     def scatter_send(k, pos, part=0, parts=1):
         rows = pl.ds(part * (half // parts), half // parts)
-        dst = nearv.at[pos - 2, rows] if k == LAYERS - 1 and pos >= 2 else precv.at[k, pos, rows]
-        return send(pbuf.at[k, pos, rows], dst, 'y' if pos % 2 else 'x', rs_send.at[k, pos, part], rs_recv.at[k, pos, part])
+        last = k == LAYERS - 1 and pos >= 2
+        dst = nearv.at[pos - 2, rows] if last else precv.at[k, pos, rows]
+        index = (pos - 2) * PARTS + part if last else 2 * PARTS + part - 1
+        sems = (rs_send.at[k, pos], rs_recv.at[k, pos]) if part == 0 and not last else (p_send.at[index], p_recv.at[index])
+        return send(pbuf.at[k, pos, rows], dst, 'y' if pos % 2 else 'x', *sems)
 
     tile_spec = pl.BlockSpec((TILE, dim), lambda t: (t, 0), pipeline_mode=DEEP)
     out_spec = pl.BlockSpec((TILE, dim), lambda t: (t, 0), pipeline_mode=OUT)
@@ -199,7 +199,7 @@
             s_ref[...] = p_ref[...] + r_ref[...]
         pltpu.emit_pipeline(body, grid=(half // TILE,), in_specs=[tile_spec] * 2, out_specs=[out_spec])(
             pbuf.at[k, 4 + h], precv.at[k, h], sbuf.at[k, h])
-        return send(sbuf.at[k, h], precv.at[k, 4 + h], 'x' if h else 'y', rs_send.at[k, 4 + h, 0], rs_recv.at[k, 4 + h, 0])
+        return send(sbuf.at[k, h], precv.at[k, 4 + h], 'x' if h else 'y', rs_send.at[k, 4 + h], rs_recv.at[k, 4 + h])
 
     def scatter_finish(k, h, near, last):
         near.wait_recv()
@@ -272,9 +272,7 @@
     item_layer(3)
 
     out_rows = (vtot[...] / (LAYERS + 1)).astype(BF16)
-    iout[...] = out_rows
-    item_done = pltpu.make_async_copy(iout, item_out, local_sem.at[2])
-    item_done.start()
+    item_out[...] = out_rows
     item_base = ((y * 2 + x) * 2 + r) * own_items
     for j in range(2):
         hit = (idcol[1 + j, :, 0:1] - item_base) == lax.broadcasted_iota(jnp.int32, (batch, own_items), 1)
@@ -310,17 +308,13 @@
     local = idcol[0, :, 0:1] - user_base
     mine[...] = jnp.zeros_like(mine)
     size = half // PARTS
-    stores = []
     for part in range(PARTS):
         rows = pl.ds(part * size, size)
         for h in (0, 1):
             parts[2 + h][part].wait_recv()
             last_user = (base[h, rows, :] + nearv[h, rows, :]).astype(BF16)
             mean = ((usum[h, rows, :] + last_user.astype(F32)) / (LAYERS + 1)).astype(BF16)
-            outv[h, rows, :] = mean
-            store = pltpu.make_async_copy(outv.at[h, rows], user_out.at[h, rows], out_sem.at[h, part])
-            store.start()
-            stores.append(store)
+            user_out[h, rows, :] = mean
             hit = (local - (h * half + part * size)) == lax.broadcasted_iota(jnp.int32, (batch, size), 1)
             mine[...] += jnp.dot(hit.astype(BF16), mean, preferred_element_type=F32)
     own_rows, other_rows = selb[r].astype(F32), selrecv[3].astype(F32)
@@ -332,9 +326,6 @@
     terms = jnp.where((local >= 0) & (local < 2 * half), soft, 0.0)
     lsend[...] = jnp.broadcast_to(jnp.sum(terms, axis=0, keepdims=True), (8, LANES))
     shared = [send_to(lsend, lrecv.at[i], device, l_send.at[i], l_recv.at[i]) for i, device in enumerate(others)]
-    for store in stores:
-        store.wait()
-    item_done.wait()
     for copy in pending:
         copy.wait_send()
     wait_all(shared)
@@ -348,7 +339,7 @@
     def device_program(mask_blk, user_shard, item_shard, triples):
         shard, dim = user_shard.shape
         half, items, own_items, batch = shard // 2, mask_blk.shape[1], item_shard.shape[0], triples.shape[0]
-        hbm = pl.BlockSpec(memory_space=pl.ANY)
+        hbm = pl.BlockSpec(memory_space=pltpu.HBM)
         vmem = pl.BlockSpec(memory_space=pltpu.VMEM)
         shapes = [((2, half, dim), BF16), ((own_items, dim), BF16), ((1, 1), F32), ((8, half, items), BF16),
                   ((LAYERS, 8, half, dim), BF16), ((LAYERS, 8, half, dim), F32), ((LAYERS, 6, half, dim), F32),
@@ -358,22 +349,22 @@
             functools.partial(kernel, (half, items, own_items, dim)),
             out_shape=[jax.ShapeDtypeStruct(*shape) for shape in shapes],
             in_specs=[hbm] * 4,
-            out_specs=[hbm, hbm, vmem] + [hbm] * 5,
+            out_specs=[vmem, vmem, vmem] + [hbm] * 5,
             scratch_shapes=[
                 pltpu.VMEM((LAYERS, 2, own_items, dim), BF16), pltpu.VMEM((2, dim, own_items), F32),
                 pltpu.VMEM((LAYERS, dim, own_items), F32), pltpu.VMEM((own_items, dim), F32),
                 pltpu.VMEM((8, 8, BUILD), F32), pltpu.VMEM((BUILD, LANES), F32), pltpu.VMEM((1, items), F32),
-                pltpu.VMEM((8, 8, BUILD), F32), pltpu.VMEM((2, 8, 8, BUILD), F32),
+                pltpu.VMEM((8, 8, BUILD), F32), pltpu.VMEM((3, 8, 8, BUILD), F32),
                 pltpu.VMEM((8, items), F32), pltpu.VMEM((8, items), F32),
                 pltpu.VMEM((2, batch, dim), BF16), pltpu.VMEM((2, batch, dim), BF16), pltpu.VMEM((4, batch, dim), BF16),
                 pltpu.VMEM((batch, dim), F32), pltpu.VMEM((8, LANES), F32), pltpu.VMEM((7, 8, LANES), F32),
                 pltpu.VMEM((3, batch), jnp.int32), pltpu.VMEM((3, batch, LANES), jnp.int32),
                 pltpu.VMEM((2, half, dim), F32), pltpu.VMEM((2, half, dim), F32), pltpu.VMEM((2, half, dim), F32),
-                pltpu.VMEM((2, half, dim), BF16), pltpu.VMEM((own_items, dim), BF16), dma((3,)), dma((2, PARTS)),
-                dma((LAYERS, 6)), dma((LAYERS, 6)), dma((LAYERS, 6, PARTS)), dma((LAYERS, 6, PARTS)), dma((LAYERS,)), dma((LAYERS,)),
-                dma((LAYERS,)), dma((LAYERS,)), dma((3,)), dma((3,)), dma((4,)), dma((4,)), dma((7,)), dma((7,))],
-            compiler_params=pltpu.CompilerParams(collective_id=0, has_side_effects=True, vmem_limit_bytes=60 * 1024 * 1024),
-        )(mask_blk, user_shard.reshape(2, half, dim), item_shard, triples.T)
+                dma((2,)),
+                dma((LAYERS, 6)), dma((LAYERS, 6)), dma((LAYERS, 6)), dma((LAYERS, 6)), dma((2 * PARTS + 1,)), dma((2 * PARTS + 1,)), dma((LAYERS,)), dma((LAYERS,)),
+                dma((LAYERS,)), dma((LAYERS,)), dma((4,)), dma((4,)), dma((4,)), dma((4,)), dma((7,)), dma((7,))],
+            compiler_params=pltpu.CompilerParams(collective_id=0, has_side_effects=True, vmem_limit_bytes=48 * 1024 * 1024),
+        )(*[pltpu.with_memory_space_constraint(a, pltpu.HBM) for a in (mask_blk, user_shard.reshape(2, half, dim), item_shard, triples.T)])
         return outs[0].reshape(shard, dim), outs[1], outs[2].reshape(())
 
     return jax.shard_map(device_program, mesh=mesh, in_specs=(P('row', COL_AXES), P(USER_AXES, None), P(ITEM_AXES, None), P()), out_specs=(P(USER_AXES, None), P(ITEM_AXES, None), P()), check_vma=False)

time: 634 us -> 628 us (level)
  no operation moved by 1% of the time
where the time goes in v3:
time: 628 us
  Pallas kernels  624 us (99%)
    pallas_call x1, Pallas kernels, device_program(): pl.pallas_call(functools.partial(kernel, (half, items, own_items, dim)),...  624 us

profile of v3, /device:TPU:0, one launch (start us, length us, event | category | flops | bytes accessed | tf_op | source)
XLA Modules:
  0.0 628.3 jit_solution(18035821982514036436)
XLA Ops:
  0.6 623.8 %shard_map.67 = (bf16[2,2048,256]{2,1,0:T(8,128)(2,1)S(1)}, bf16[1024,256]{1,0:T(8,128)(2,1)S(1)}, f32[1,1]{1,0:T(1,128)}, bf16[8,2048,2048]{2,1,0:T(8,128)(2,1)...) custom-call(s32[16384,2048]{1,0:T(8,128)} %mask.1, ...), custom_call_target="tpu_custom_call" | custom-call | tf_op jit(solution)/shard_map/pallas_call | solution.py:348
  624.4 1.3 copy.10
  625.8 0.8 copy.11

commit v4 on v3

--- a/solution.py
+++ b/solution.py
@@ -26,7 +26,7 @@
 
 
 def kernel(dims, mask, user0, item0, triples, user_out, item_out, loss_out, adj, upan, pbuf, precv, sbuf,
-           vpan, acc, qrecv, vtot, us, uscol, isc, degu, drecv, degi, degi_recv, sel, selb, selrecv, mine, lsend, lrecv,
+           vpan, acc, qrecv, vtot, us, uscol, isc, degu, dsend, drecv, degi, degi_recv, sel, selb, selrecv, mine, lsend, lrecv,
            ids, idcol, base, usum, nearv, local_sem,
            ag_send, ag_recv, rs_send, rs_recv, p_send, p_recv, v_send, v_recv, q_send, q_recv, d_send, d_recv, e_send, e_recv, l_send, l_recv):
     half, items, own_items, dim = dims
@@ -118,15 +118,20 @@
     pltpu.emit_pipeline(degree_body, grid=(8, half // BUILD),
                         in_specs=[pl.BlockSpec((BUILD, items), lambda p, t: (mask_block(p, t), 0), pipeline_mode=DEEP)])(mask)
     item_deg = send(degi, degi_recv, 'r', d_send.at[0], d_recv.at[0])
-    user_deg = [send(degu, drecv.at[i], direction, d_send.at[1 + i], d_recv.at[1 + i]) for i, direction in enumerate(('x', 'y', 'xy'))]
+    for q in range(4):
+        pair = jnp.concatenate([degu[2 * q], degu[2 * q + 1]], axis=0)
+        dsend[q] = pair.astype(jnp.int32).astype(jnp.int16)
+    user_deg = [send(dsend, drecv.at[i], direction, d_send.at[1 + i], d_recv.at[1 + i]) for i, direction in enumerate(('x', 'y', 'xy'))]
     rest0 = gather_forward(0, gather0)
     item_deg.wait_recv()
     total = jnp.sum(degi[...] + degi_recv[...], axis=0, keepdims=True)
     isc[...] = lax.rsqrt(jnp.maximum(total, 1.0))
     wait_all(user_deg)
     for pos in range(8):
-        flips = (2, 4, 6) if pos % 2 else (4, 2, 6)
-        count = (degu[pos] + drecv[0, pos ^ flips[0]]) + (drecv[1, pos ^ flips[1]] + drecv[2, pos ^ flips[2]])
+        count = degu[pos]
+        for i, flip in enumerate((2, 4, 6) if pos % 2 else (4, 2, 6)):
+            part = drecv[i, (pos ^ flip) // 2].astype(jnp.int32)
+            count = count + part[pos % 2 * 8:pos % 2 * 8 + 8].astype(F32)
         us[pos] = lax.rsqrt(jnp.maximum(count, 1.0))
     item_copy.wait_recv()
 
@@ -354,7 +359,7 @@
                 pltpu.VMEM((LAYERS, 2, own_items, dim), BF16), pltpu.VMEM((2, dim, own_items), F32),
                 pltpu.VMEM((LAYERS, dim, own_items), F32), pltpu.VMEM((own_items, dim), F32),
                 pltpu.VMEM((8, 8, BUILD), F32), pltpu.VMEM((BUILD, LANES), F32), pltpu.VMEM((1, items), F32),
-                pltpu.VMEM((8, 8, BUILD), F32), pltpu.VMEM((3, 8, 8, BUILD), F32),
+                pltpu.VMEM((8, 8, BUILD), F32), pltpu.VMEM((4, 16, BUILD), jnp.int16), pltpu.VMEM((3, 4, 16, BUILD), jnp.int16),
                 pltpu.VMEM((8, items), F32), pltpu.VMEM((8, items), F32),
                 pltpu.VMEM((2, batch, dim), BF16), pltpu.VMEM((2, batch, dim), BF16), pltpu.VMEM((4, batch, dim), BF16),
                 pltpu.VMEM((batch, dim), F32), pltpu.VMEM((8, LANES), F32), pltpu.VMEM((7, 8, LANES), F32),

time: 628 us -> 627 us (level)
  no operation moved by 1% of the time
where the time goes in v4:
time: 627 us
  Pallas kernels  622 us (99%)
    pallas_call x1, Pallas kernels, device_program(): pl.pallas_call(functools.partial(kernel, (half, items, own_items, dim)),...  622 us

profile of v4, /device:TPU:0, one launch (start us, length us, event | category | flops | bytes accessed | tf_op | source)
XLA Modules:
  0.0 626.9 jit_solution(10334426262665585049)
XLA Ops:
  0.6 622.4 %shard_map.67 = (bf16[2,2048,256]{2,1,0:T(8,128)(2,1)S(1)}, bf16[1024,256]{1,0:T(8,128)(2,1)S(1)}, f32[1,1]{1,0:T(1,128)}, bf16[8,2048,2048]{2,1,0:T(8,128)(2,1)...) custom-call(s32[16384,2048]{1,0:T(8,128)} %mask.1, ...), custom_call_target="tpu_custom_call" | custom-call | tf_op jit(solution)/shard_map/pallas_call | solution.py:353
  623.0 1.3 copy.10
  624.4 0.8 copy.11

commit v5 on v3

--- a/solution.py
+++ b/solution.py
@@ -20,6 +20,7 @@
 TILE = 512
 CHUNK = 32
 PARTS = 4
+HEAD = 256
 DEEP = pl.Buffered(4)
 OUT = pl.Buffered(2)
 LANES = 128
@@ -118,16 +119,24 @@
     pltpu.emit_pipeline(degree_body, grid=(8, half // BUILD),
                         in_specs=[pl.BlockSpec((BUILD, items), lambda p, t: (mask_block(p, t), 0), pipeline_mode=DEEP)])(mask)
     item_deg = send(degi, degi_recv, 'r', d_send.at[0], d_recv.at[0])
-    user_deg = [send(degu, drecv.at[i], direction, d_send.at[1 + i], d_recv.at[1 + i]) for i, direction in enumerate(('x', 'y', 'xy'))]
-    rest0 = gather_forward(0, gather0)
+    user_deg = send(degu, drecv.at[0], 'x', d_send.at[1], d_recv.at[1])
+    head, tail = pl.ds(0, HEAD), pl.ds(HEAD, half - HEAD)
+    gather0[0].wait_recv()
+    rest0 = gather0[2:] + [send(upan.at[0, 2, head], upan.at[0, 0, head], 'y', ag_send.at[0, 4], ag_recv.at[0, 4])]
+    gather0[1].wait_recv()
+    rest0.append(send(upan.at[0, 3], upan.at[0, 1], 'x', ag_send.at[0, 5], ag_recv.at[0, 5]))
+    user_deg.wait_recv()
+    for pos in range(8):
+        us[pos] = degu[pos] + drecv[0, pos ^ (2 if pos % 2 else 4)]
+    user_deg2 = send(us, drecv.at[1], 'y', d_send.at[2], d_recv.at[2])
+    rest0.append(send(upan.at[0, 2, tail], upan.at[0, 0, tail], 'y', d_send.at[3], d_recv.at[3]))
     item_deg.wait_recv()
     total = jnp.sum(degi[...] + degi_recv[...], axis=0, keepdims=True)
     isc[...] = lax.rsqrt(jnp.maximum(total, 1.0))
-    wait_all(user_deg)
+    user_deg2.wait_recv()
+    finish(user_deg)
     for pos in range(8):
-        flips = (2, 4, 6) if pos % 2 else (4, 2, 6)
-        count = (degu[pos] + drecv[0, pos ^ flips[0]]) + (drecv[1, pos ^ flips[1]] + drecv[2, pos ^ flips[2]])
-        us[pos] = lax.rsqrt(jnp.maximum(count, 1.0))
+        degu[pos] = lax.rsqrt(jnp.maximum(us[pos] + drecv[1, pos ^ (4 if pos % 2 else 2)], 1.0))
     item_copy.wait_recv()
 
     def panel(k):
@@ -142,7 +151,7 @@
         def body(m_ref, *refs):
             (u_ref, a_ref, p_ref) = refs if users is not None else (None,) + refs
             pos, tile = pl.program_id(0) + first, pl.program_id(1) + start_tile
-            row = us[pos, pl.ds(tile, 1), :]
+            row = degu[pos, pl.ds(tile, 1), :]
             uscol[...] = jnp.transpose(jnp.broadcast_to(row, (LANES, BUILD)))
 
             def chunk(i, carry):
@@ -354,7 +363,7 @@
                 pltpu.VMEM((LAYERS, 2, own_items, dim), BF16), pltpu.VMEM((2, dim, own_items), F32),
                 pltpu.VMEM((LAYERS, dim, own_items), F32), pltpu.VMEM((own_items, dim), F32),
                 pltpu.VMEM((8, 8, BUILD), F32), pltpu.VMEM((BUILD, LANES), F32), pltpu.VMEM((1, items), F32),
-                pltpu.VMEM((8, 8, BUILD), F32), pltpu.VMEM((3, 8, 8, BUILD), F32),
+                pltpu.VMEM((8, 8, BUILD), F32), pltpu.VMEM((2, 8, 8, BUILD), F32),
                 pltpu.VMEM((8, items), F32), pltpu.VMEM((8, items), F32),
                 pltpu.VMEM((2, batch, dim), BF16), pltpu.VMEM((2, batch, dim), BF16), pltpu.VMEM((4, batch, dim), BF16),
                 pltpu.VMEM((batch, dim), F32), pltpu.VMEM((8, LANES), F32), pltpu.VMEM((7, 8, LANES), F32),

time: 628 us -> 627 us (level)
  no operation moved by 1% of the time
where the time goes in v5:
time: 627 us
  Pallas kernels  623 us (99%)
    pallas_call x1, Pallas kernels, device_program(): pl.pallas_call(functools.partial(kernel, (half, items, own_items, dim)),...  623 us

profile of v5, /device:TPU:0, one launch (start us, length us, event | category | flops | bytes accessed | tf_op | source)
XLA Modules:
  0.0 627.3 jit_solution(248280550908033282)
XLA Ops:
  0.6 622.8 %shard_map.67 = (bf16[2,2048,256]{2,1,0:T(8,128)(2,1)S(1)}, bf16[1024,256]{1,0:T(8,128)(2,1)S(1)}, f32[1,1]{1,0:T(1,128)}, bf16[8,2048,2048]{2,1,0:T(8,128)(2,1)...) custom-call(s32[16384,2048]{1,0:T(8,128)} %mask.1, ...), custom_call_target="tpu_custom_call" | custom-call | tf_op jit(solution)/shard_map/pallas_call | solution.py:357
  623.4 1.3 copy.10
  624.7 0.8 copy.11

commit v6 on v5

--- a/solution.py
+++ b/solution.py
@@ -20,7 +20,7 @@
 TILE = 512
 CHUNK = 32
 PARTS = 4
-HEAD = 256
+HEAD = 320
 DEEP = pl.Buffered(4)
 OUT = pl.Buffered(2)
 LANES = 128

time: 627 us -> 627 us (level)
  no operation moved by 1% of the time
where the time goes in v6:
time: 627 us
  Pallas kernels  622 us (99%)
    pallas_call x1, Pallas kernels, device_program(): pl.pallas_call(functools.partial(kernel, (half, items, own_items, dim)),...  622 us

profile of v6, /device:TPU:0, one launch (start us, length us, event | category | flops | bytes accessed | tf_op | source)
XLA Modules:
  0.0 626.9 jit_solution(5904584990896274035)
XLA Ops:
  0.6 622.4 %shard_map.67 = (bf16[2,2048,256]{2,1,0:T(8,128)(2,1)S(1)}, bf16[1024,256]{1,0:T(8,128)(2,1)S(1)}, f32[1,1]{1,0:T(1,128)}, bf16[8,2048,2048]{2,1,0:T(8,128)(2,1)...) custom-call(s32[16384,2048]{1,0:T(8,128)} %mask.1, ...), custom_call_target="tpu_custom_call" | custom-call | tf_op jit(solution)/shard_map/pallas_call | solution.py:357
  623.0 1.3 copy.10
  624.4 0.8 copy.11

commit v7 on v6

--- a/solution.py
+++ b/solution.py
@@ -29,7 +29,7 @@
 def kernel(dims, mask, user0, item0, triples, user_out, item_out, loss_out, adj, upan, pbuf, precv, sbuf,
            vpan, acc, qrecv, vtot, us, uscol, isc, degu, drecv, degi, degi_recv, sel, selb, selrecv, mine, lsend, lrecv,
            ids, idcol, base, usum, nearv, local_sem,
-           ag_send, ag_recv, rs_send, rs_recv, p_send, p_recv, v_send, v_recv, q_send, q_recv, d_send, d_recv, e_send, e_recv, l_send, l_recv):
+           ag_send, ag_recv, rs_send, rs_recv, p_recv, v_send, v_recv, q_send, q_recv, d_send, d_recv, e_send, e_recv, l_send, l_recv):
     half, items, own_items, dim = dims
     x, y, r = lax.axis_index('colb'), lax.axis_index('cola'), lax.axis_index('row')
     to = {'x': {'colb': 1 - x}, 'y': {'cola': 1 - y}, 'r': {'row': 1 - r},
@@ -39,15 +39,20 @@
     pending = []
     batch = ids.shape[1]
 
-    def send_to(src, dst, device, send_sem, recv_sem):
+    def send_to(src, dst, device, send_sem, recv_sem, shared=False):
         copy = pltpu.make_async_remote_copy(src_ref=src, dst_ref=dst, send_sem=send_sem, recv_sem=recv_sem,
                                             device_id=device, device_id_type=pl.DeviceIdType.MESH)
         copy.start()
-        pending.append(copy)
+        if not shared:
+            pending.append(copy)
         return copy
 
-    def send(src, dst, direction, send_sem, recv_sem):
-        return send_to(src, dst, to[direction], send_sem, recv_sem)
+    def send(src, dst, direction, send_sem, recv_sem, shared=False):
+        return send_to(src, dst, to[direction], send_sem, recv_sem, shared)
+
+    def wait_sent(ref, send_sem, recv_sem):
+        pltpu.make_async_remote_copy(src_ref=ref, dst_ref=ref, send_sem=send_sem, recv_sem=recv_sem,
+                                     device_id=to['x'], device_id_type=pl.DeviceIdType.MESH).wait_send()
 
     def finish(copy):
         copy.wait_send()
@@ -66,16 +71,16 @@
         return user0.at[h] if k == 0 else upan.at[k, 6 + h]
 
     def gather_start(k):
-        return [send(own(k, 0), upan.at[k, 2], 'x', ag_send.at[k, 0], ag_recv.at[k, 0]),
-                send(own(k, 1), upan.at[k, 3], 'y', ag_send.at[k, 1], ag_recv.at[k, 1]),
-                send(own(k, 0), upan.at[k, 4], 'y', ag_send.at[k, 2], ag_recv.at[k, 2]),
-                send(own(k, 1), upan.at[k, 5], 'x', ag_send.at[k, 3], ag_recv.at[k, 3])]
+        return [send(own(k, 0), upan.at[k, 2], 'x', ag_send.at[k], ag_recv.at[k, 0], True),
+                send(own(k, 1), upan.at[k, 3], 'y', ag_send.at[k], ag_recv.at[k, 1], True),
+                send(own(k, 0), upan.at[k, 4], 'y', ag_send.at[k], ag_recv.at[k, 2], True),
+                send(own(k, 1), upan.at[k, 5], 'x', ag_send.at[k], ag_recv.at[k, 3], True)]
 
     def gather_forward(k, copies):
         copies[0].wait_recv()
-        far0 = send(upan.at[k, 2], upan.at[k, 0], 'y', ag_send.at[k, 4], ag_recv.at[k, 4])
+        far0 = send(upan.at[k, 2], upan.at[k, 0], 'y', ag_send.at[k], ag_recv.at[k, 4], True)
         copies[1].wait_recv()
-        far1 = send(upan.at[k, 3], upan.at[k, 1], 'x', ag_send.at[k, 5], ag_recv.at[k, 5])
+        far1 = send(upan.at[k, 3], upan.at[k, 1], 'x', ag_send.at[k], ag_recv.at[k, 5], True)
         return copies[2:] + [far0, far1]
 
     def wait_all(copies):
@@ -122,14 +127,14 @@
     user_deg = send(degu, drecv.at[0], 'x', d_send.at[1], d_recv.at[1])
     head, tail = pl.ds(0, HEAD), pl.ds(HEAD, half - HEAD)
     gather0[0].wait_recv()
-    rest0 = gather0[2:] + [send(upan.at[0, 2, head], upan.at[0, 0, head], 'y', ag_send.at[0, 4], ag_recv.at[0, 4])]
+    rest0 = gather0[2:] + [send(upan.at[0, 2, head], upan.at[0, 0, head], 'y', ag_send.at[0], ag_recv.at[0, 4], True)]
     gather0[1].wait_recv()
-    rest0.append(send(upan.at[0, 3], upan.at[0, 1], 'x', ag_send.at[0, 5], ag_recv.at[0, 5]))
+    rest0.append(send(upan.at[0, 3], upan.at[0, 1], 'x', ag_send.at[0], ag_recv.at[0, 5], True))
     user_deg.wait_recv()
     for pos in range(8):
         us[pos] = degu[pos] + drecv[0, pos ^ (2 if pos % 2 else 4)]
     user_deg2 = send(us, drecv.at[1], 'y', d_send.at[2], d_recv.at[2])
-    rest0.append(send(upan.at[0, 2, tail], upan.at[0, 0, tail], 'y', d_send.at[3], d_recv.at[3]))
+    rest0.append(send(upan.at[0, 2, tail], upan.at[0, 0, tail], 'y', ag_send.at[0], d_recv.at[3], True))
     item_deg.wait_recv()
     total = jnp.sum(degi[...] + degi_recv[...], axis=0, keepdims=True)
     isc[...] = lax.rsqrt(jnp.maximum(total, 1.0))
@@ -195,8 +200,8 @@
         last = k == LAYERS - 1 and pos >= 2
         dst = nearv.at[pos - 2, rows] if last else precv.at[k, pos, rows]
         index = (pos - 2) * PARTS + part if last else 2 * PARTS + part - 1
-        sems = (rs_send.at[k, pos], rs_recv.at[k, pos]) if part == 0 and not last else (p_send.at[index], p_recv.at[index])
-        return send(pbuf.at[k, pos, rows], dst, 'y' if pos % 2 else 'x', *sems)
+        recv_sem = rs_recv.at[k, pos] if part == 0 and not last else p_recv.at[index]
+        return send(pbuf.at[k, pos, rows], dst, 'y' if pos % 2 else 'x', rs_send.at[k], recv_sem, True)
 
     tile_spec = pl.BlockSpec((TILE, dim), lambda t: (t, 0), pipeline_mode=DEEP)
     out_spec = pl.BlockSpec((TILE, dim), lambda t: (t, 0), pipeline_mode=OUT)
@@ -208,7 +213,7 @@
             s_ref[...] = p_ref[...] + r_ref[...]
         pltpu.emit_pipeline(body, grid=(half // TILE,), in_specs=[tile_spec] * 2, out_specs=[out_spec])(
             pbuf.at[k, 4 + h], precv.at[k, h], sbuf.at[k, h])
-        return send(sbuf.at[k, h], precv.at[k, 4 + h], 'x' if h else 'y', rs_send.at[k, 4 + h], rs_recv.at[k, 4 + h])
+        return send(sbuf.at[k, h], precv.at[k, 4 + h], 'x' if h else 'y', rs_send.at[k], rs_recv.at[k, 4 + h], True)
 
     def scatter_finish(k, h, near, last):
         near.wait_recv()
@@ -334,9 +339,13 @@
     soft = jnp.maximum(-margin, 0.0) + jnp.log1p(jnp.exp(-jnp.abs(margin)))
     terms = jnp.where((local >= 0) & (local < 2 * half), soft, 0.0)
     lsend[...] = jnp.broadcast_to(jnp.sum(terms, axis=0, keepdims=True), (8, LANES))
-    shared = [send_to(lsend, lrecv.at[i], device, l_send.at[i], l_recv.at[i]) for i, device in enumerate(others)]
+    shared = [send_to(lsend, lrecv.at[i], device, l_send, l_recv.at[i], True) for i, device in enumerate(others)]
     for copy in pending:
         copy.wait_send()
+    for k in range(LAYERS):
+        wait_sent(upan.at[k, pl.ds(0, 6)], ag_send.at[k], ag_recv.at[k, 0])
+        wait_sent(pbuf.at[k, pl.ds(0, 6)], rs_send.at[k], rs_recv.at[k, 0])
+    wait_sent(lrecv, l_send, l_recv.at[0])
     wait_all(shared)
     level = [lsend[...]] + [lrecv[i] for i in range(len(others))]
     while len(level) > 1:
@@ -370,8 +379,8 @@
                 pltpu.VMEM((3, batch), jnp.int32), pltpu.VMEM((3, batch, LANES), jnp.int32),
                 pltpu.VMEM((2, half, dim), F32), pltpu.VMEM((2, half, dim), F32), pltpu.VMEM((2, half, dim), F32),
                 dma((2,)),
-                dma((LAYERS, 6)), dma((LAYERS, 6)), dma((LAYERS, 6)), dma((LAYERS, 6)), dma((2 * PARTS + 1,)), dma((2 * PARTS + 1,)), dma((LAYERS,)), dma((LAYERS,)),
-                dma((LAYERS,)), dma((LAYERS,)), dma((4,)), dma((4,)), dma((4,)), dma((4,)), dma((7,)), dma((7,))],
+                dma((LAYERS,)), dma((LAYERS, 6)), dma((LAYERS,)), dma((LAYERS, 6)), dma((2 * PARTS + 1,)), dma((LAYERS,)), dma((LAYERS,)),
+                dma((LAYERS,)), dma((LAYERS,)), dma((4,)), dma((4,)), dma((4,)), dma((4,)), dma(()), dma((7,))],
             compiler_params=pltpu.CompilerParams(collective_id=0, has_side_effects=True, vmem_limit_bytes=48 * 1024 * 1024),
         )(*[pltpu.with_memory_space_constraint(a, pltpu.HBM) for a in (mask_blk, user_shard.reshape(2, half, dim), item_shard, triples.T)])
         return outs[0].reshape(shard, dim), outs[1], outs[2].reshape(())

time: 627 us -> 627 us (level)
  no operation moved by 1% of the time
where the time goes in v7:
time: 627 us
  Pallas kernels  622 us (99%)
    pallas_call x1, Pallas kernels, device_program(): pl.pallas_call(functools.partial(kernel, (half, items, own_items, dim)),...  622 us

profile of v7, /device:TPU:0, one launch (start us, length us, event | category | flops | bytes accessed | tf_op | source)
XLA Modules:
  0.0 626.5 jit_solution(11445038068712832443)
XLA Ops:
  0.6 622.0 %shard_map.67 = (bf16[2,2048,256]{2,1,0:T(8,128)(2,1)S(1)}, bf16[1024,256]{1,0:T(8,128)(2,1)S(1)}, f32[1,1]{1,0:T(1,128)}, bf16[8,2048,2048]{2,1,0:T(8,128)(2,1)...) custom-call(s32[16384,2048]{1,0:T(8,128)} %mask.1, ...), custom_call_target="tpu_custom_call" | custom-call | tf_op jit(solution)/shard_map/pallas_call | solution.py:366
  622.6 1.3 copy.10
  624.0 0.8 copy.11

commit v8 on v7

--- a/solution.py
+++ b/solution.py
@@ -338,7 +338,7 @@
     margin = (jnp.sum(rows * pos_rows, axis=1, keepdims=True) - jnp.sum(rows * neg_rows, axis=1, keepdims=True)) / math.sqrt(dim)
     soft = jnp.maximum(-margin, 0.0) + jnp.log1p(jnp.exp(-jnp.abs(margin)))
     terms = jnp.where((local >= 0) & (local < 2 * half), soft, 0.0)
-    lsend[...] = jnp.broadcast_to(jnp.sum(terms, axis=0, keepdims=True), (8, LANES))
+    lsend[...] = jnp.broadcast_to(jnp.sum(terms, axis=0, keepdims=True), (1, LANES))
     shared = [send_to(lsend, lrecv.at[i], device, l_send, l_recv.at[i], True) for i, device in enumerate(others)]
     for copy in pending:
         copy.wait_send()
@@ -375,7 +375,7 @@
                 pltpu.VMEM((8, 8, BUILD), F32), pltpu.VMEM((2, 8, 8, BUILD), F32),
                 pltpu.VMEM((8, items), F32), pltpu.VMEM((8, items), F32),
                 pltpu.VMEM((2, batch, dim), BF16), pltpu.VMEM((2, batch, dim), BF16), pltpu.VMEM((4, batch, dim), BF16),
-                pltpu.VMEM((batch, dim), F32), pltpu.VMEM((8, LANES), F32), pltpu.VMEM((7, 8, LANES), F32),
+                pltpu.VMEM((batch, dim), F32), pltpu.VMEM((1, LANES), F32), pltpu.VMEM((7, 1, LANES), F32),
                 pltpu.VMEM((3, batch), jnp.int32), pltpu.VMEM((3, batch, LANES), jnp.int32),
                 pltpu.VMEM((2, half, dim), F32), pltpu.VMEM((2, half, dim), F32), pltpu.VMEM((2, half, dim), F32),
                 dma((2,)),

time: 627 us -> 627 us (level)
  no operation moved by 1% of the time
where the time goes in v8:
time: 627 us; the launch traced here: 626 us
  Pallas kernels  622 us (99%)
    pallas_call x1, Pallas kernels, device_program(): pl.pallas_call(functools.partial(kernel, (half, items, own_items, dim)),...  622 us

profile of v8, /device:TPU:0, one launch (start us, length us, event | category | flops | bytes accessed | tf_op | source)
XLA Modules:
  0.0 626.4 jit_solution(7314882631847597321)
XLA Ops:
  0.6 621.9 %shard_map.67 = (bf16[2,2048,256]{2,1,0:T(8,128)(2,1)S(1)}, bf16[1024,256]{1,0:T(8,128)(2,1)S(1)}, f32[1,1]{1,0:T(1,128)}, bf16[8,2048,2048]{2,1,0:T(8,128)(2,1)...) custom-call(s32[16384,2048]{1,0:T(8,128)} %mask.1, ...), custom_call_target="tpu_custom_call" | custom-call | tf_op jit(solution)/shard_map/pallas_call | solution.py:366
  622.6 1.3 copy.10
  623.9 0.8 copy.11
